TPU v7x, 256 devices: a whole 4x4x8 slice. The times are simulated.
256 devices in a mesh: fsdp: 128 (over z, x, y), dp: 2 (over core).
Axes of the slice: x: 4, y: 4, z: 8, core: 2. Of those that a mesh axis runs over, the one named last changes fastest.
Arguments:
- gradients: bfloat16 [2, 512, 256, 256], P('dp', 'fsdp'), may hold values from -6 to 6
- first_moment: float32 [768, 256, 256], P('fsdp'), may hold values from -4 to 4
- second_moment: float32 [768, 256, 256], P('fsdp'), may hold values from 0.05 to 2
- left_basis: float32 [768, 256, 256], P('fsdp'), may hold values from -1 to 1, as said below
- right_basis: float32 [768, 256, 256], P('fsdp'), may hold values from -1 to 1, as said below
- shard_starts: int32 [128], replicated, may hold values from 0 to 384, as said below
- block_owners: int32 [384], replicated, may hold values from 0 to 127, as said below
Outputs:
- direction: float32 [512, 256, 256], P('fsdp')
- first_new: float32 [768, 256, 256], P('fsdp')
- second_new: float32 [768, 256, 256], P('fsdp')
Inputs may be any that keep to these rules, and one draw needn't show every extreme that they name: Starts never fall and shard_starts[0] = 0; a device holds at most 4 blocks, some device exactly 4 and some none. `block_owners`: never falls; a device owns at most 6 blocks, some device exactly 6 and some none; a block's owner differs from its holder by at most 2 fsdp indices, by exactly 2 for some block in each direction. `left_basis`: each matrix is orthogonal up to float32 rounding. `right_basis`: each matrix is orthogonal up to float32 rounding.
All inputs are finite; a program needn't handle non-finite values.
Results may differ from a plain program's by a relative error of at most 0.0014.
Values may be sent and summed in bfloat16 or wider, within the bound.
A program may use at most 64 MiB of HBM per device.

v0:
```python
import jax
import jax.numpy as jnp
from jax import lax
from jax.sharding import PartitionSpec as P

REACH = 2
STEP = 10


beta_one = 0.9
beta_two = 0.95
epsilon = 1e-08


def in_blocks(x, dim, length):
    before, after = (x.shape[:dim], x.shape[dim + 1 :])
    return jnp.moveaxis(x.reshape(*before, length, -1, *after), dim, 0)


def summed_on_arrival(x, axis, dim):
    blocks = in_blocks(x, dim, lax.axis_size(axis))
    arrived = lax.all_to_all(blocks, axis, split_axis=0, concat_axis=0, tiled=True)
    return arrived.astype(jnp.float32).sum(axis=0)


def from_behind(value, axis, steps):
    count = lax.axis_size(axis)
    initial, last = (max(0, -steps), min(count, count - steps))
    return lax.ppermute(value, axis, [(source, source + steps) for source in range(initial, last)])


def sent_to_all(x, axis):
    length = lax.axis_size(axis)
    return lax.all_to_all(jnp.broadcast_to(x[None], (length, *x.shape)), axis, 0, 0, tiled=True)


def joined_along(blocks, dim):
    blocks = jnp.moveaxis(blocks, 0, dim)
    shape = blocks.shape
    return blocks.reshape(*shape[:dim], shape[dim] * shape[dim + 1], *shape[dim + 2 :])


def gather_directly(x, axis, dim):
    blocks = sent_to_all(x, axis)
    return joined_along(blocks, dim)


def soap_blocks(gradient, moment_one, moment_two, left_basis, right_basis):
    highest = lax.Precision.HIGHEST
    moment_new = beta_one * moment_one + (1.0 - beta_one) * gradient
    turned = jnp.einsum(
        "jad,jde->jae",
        jnp.einsum("jba,jbd->jad", left_basis, gradient, precision=highest),
        right_basis,
        precision=highest,
    )
    turned_moment = jnp.einsum(
        "jad,jde->jae",
        jnp.einsum("jba,jbd->jad", left_basis, moment_new, precision=highest),
        right_basis,
        precision=highest,
    )
    second_next = beta_two * moment_two + (1.0 - beta_two) * turned * turned
    bias_one = 1.0 - beta_one**STEP
    bias_two = 1.0 - beta_two**STEP
    scaled = turned_moment / bias_one / (jnp.sqrt(second_next / bias_two) + epsilon)
    update = jnp.einsum(
        "jad,jed->jae",
        jnp.einsum("jab,jbd->jad", left_basis, scaled, precision=highest),
        right_basis,
        precision=highest,
    )
    return (moment_new, second_next, update)


def layout(shard_starts, block_owners, devices):
    total_blocks = block_owners.shape[0]
    ends = jnp.concatenate([shard_starts[1:], jnp.full((1,), total_blocks, jnp.int32)])
    held_counts = ends - shard_starts
    device_ids = jnp.arange(devices, dtype=jnp.int32)
    own_counts = jnp.sum((block_owners[None, :] == device_ids[:, None]).astype(jnp.int32), axis=1)
    firsts = jnp.cumsum(own_counts) - own_counts
    return (held_counts, own_counts, firsts)


def linking(own_first, own_count, hold_start, hold_count, in_range, slot_count, owned_slots):
    owner_pos = own_first + jnp.arange(owned_slots, dtype=jnp.int32)
    holder_pos = hold_start + jnp.arange(slot_count, dtype=jnp.int32)
    live_pair = (
        (jnp.arange(owned_slots)[:, None] < own_count)
        & (jnp.arange(slot_count)[None, :] < hold_count)
        & in_range
    )
    return (owner_pos[:, None] == holder_pos[None, :]) & live_pair


def body(
    gradients, first_moment, second_moment, left_basis, right_basis, shard_starts, block_owners
):
    devices = lax.axis_size("fsdp")
    myself = lax.axis_index("fsdp")
    slot_count = gradients.shape[1]
    owned_slots = first_moment.shape[0]
    block_width = gradients.shape[3]
    held_counts, own_counts, firsts = layout(shard_starts, block_owners, devices)
    summed = summed_on_arrival(
        gradients[0].astype(jnp.float32).astype(jnp.bfloat16), "dp", 1
    ).astype(jnp.bfloat16)
    assembled = jnp.zeros((owned_slots, summed.shape[1], block_width), jnp.float32)
    for offset in range(-REACH, REACH + 1):
        source = myself - offset
        if offset == 0:
            arriving = summed
        else:
            arriving = from_behind(summed, "fsdp", offset)
        in_range = (source >= 0) & (source < devices)
        picked = jnp.clip(source, 0, devices - 1)
        matching = linking(
            firsts[myself],
            own_counts[myself],
            shard_starts[picked],
            held_counts[picked],
            in_range,
            slot_count,
            owned_slots,
        )
        assembled = assembled + jnp.einsum(
            "js,sab->jab",
            matching.astype(jnp.bfloat16),
            arriving,
            preferred_element_type=jnp.float32,
        )
    gradient = gather_directly(assembled.astype(jnp.bfloat16), "dp", 1).astype(jnp.float32)
    own_live = own_counts[myself]
    moment_new, second_next, update = soap_blocks(
        gradient, first_moment, second_moment, left_basis, right_basis
    )
    live_slots = (jnp.arange(owned_slots) < own_live)[:, None, None]
    moment_new = jnp.where(live_slots, moment_new, 0.0)
    second_next = jnp.where(live_slots, second_next, 0.0)
    update = jnp.where(live_slots, update, 0.0)
    half_rows = block_width // lax.axis_size("dp")
    sending = lax.dynamic_slice_in_dim(update, lax.axis_index("dp") * half_rows, half_rows, 1)
    collected = jnp.zeros((slot_count, sending.shape[1], block_width), jnp.float32)
    for offset in range(-REACH, REACH + 1):
        source = myself + offset
        if offset == 0:
            arriving = sending
        else:
            arriving = from_behind(sending, "fsdp", -offset)
        in_range = (source >= 0) & (source < devices)
        picked = jnp.clip(source, 0, devices - 1)
        matching = linking(
            firsts[picked],
            own_counts[picked],
            shard_starts[myself],
            held_counts[myself],
            in_range,
            slot_count,
            owned_slots,
        )
        collected = collected + jnp.einsum(
            "js,jab->sab", matching.astype(jnp.float32), arriving, precision=lax.Precision.HIGHEST
        )
    direction = gather_directly(collected, "dp", 1)
    return (direction, moment_new, second_next)


def solution(mesh):
    in_specs = (
        P("dp", "fsdp", None, None),
        P("fsdp", None, None),
        P("fsdp", None, None),
        P("fsdp", None, None),
        P("fsdp", None, None),
        P(),
        P(),
    )
    out_specs = (P("fsdp", None, None), P("fsdp", None, None), P("fsdp", None, None))
    return jax.shard_map(body, mesh=mesh, in_specs=in_specs, out_specs=out_specs, check_vma=False)
```

profile of v0, /device:TPU:103, one launch (start us, length us, event | category | flops | bytes accessed | tf_op | source)
XLA Modules:
  0.0 151.4 jit_solution(7168354181356780548)
XLA Ops:
  0.7 1.2 copy.71
  1.9 4.5 %all_to_all.15 = bf16[2,4,128,256]{3,2,1,0:T(8,128)(2,1)S(1)} all-to-all(bf16[2,4,128,256]{3,2,1,0:T(8,128)(2,1)S(1)} %copy.71), channel_id=1, replica_groups=mesh['fsdp'=128,'dp'=2] {'dp'}, dimensions={0} | all-to-all | bytes 1048576 | tf_op jit(solution)/shard_map/all_to_all | solution.py:22
  7.4 4.9 %collective-permute-start.1 = (bf16[4,128,256]{2,0,1:T(4,128)(2,1)}, bf16[4,128,256]{2,0,1:T(4,128)(2,1)}, u32[]{:S(2)}, u32[]{:S(2)}) collective-permute-start(bf16[4,128,256]{2,0,1:T(4,128)(2,1)} %copy.73), channel_id=1, source_target_pairs={{2,0},{4,2},{6,4},{8,6},{10,8},{12,10},{14,12},{16,14},{18,16},{20... | collective-permute-start | bytes 786440 | tf_op jit(solution)/shard_map/ppermute | solution.py:29
  12.3 2.3 %collective-permute-start = (bf16[4,128,256]{2,0,1:T(4,128)(2,1)}, bf16[4,128,256]{2,0,1:T(4,128)(2,1)S(1)}, u32[]{:S(2)}, u32[]{:S(2)}) collective-permute-start(bf16[4,128,256]{2,0,1:T(4,128)(2,1)} %copy.73), channel_id=1, source_target_pairs={{4,0},{6,2},{8,4},{10,6},{12,8},{14,10},{16,12},{18,14},{20,16},{2... | collective-permute-start | bytes 786440 | tf_op jit(solution)/shard_map/ppermute | solution.py:29
  14.6 4.5 %collective-permute-start.3 = (bf16[4,128,256]{2,0,1:T(4,128)(2,1)}, bf16[4,128,256]{2,0,1:T(4,128)(2,1)S(1)}, u32[]{:S(2)}, u32[]{:S(2)}) collective-permute-start(bf16[4,128,256]{2,0,1:T(4,128)(2,1)} %copy.73), channel_id=1, source_target_pairs={{0,4},{2,6},{4,8},{6,10},{8,12},{10,14},{12,16},{14,18},{16,20},{1... | collective-permute-start | bytes 786440 | tf_op jit(solution)/shard_map/ppermute | solution.py:29
  19.1 1.9 %collective-permute-start.2 = (bf16[4,128,256]{2,0,1:T(4,128)(2,1)}, bf16[4,128,256]{2,0,1:T(4,128)(2,1)}, u32[]{:S(2)}, u32[]{:S(2)}) collective-permute-start(bf16[4,128,256]{2,0,1:T(4,128)(2,1)} %copy.73), channel_id=1, source_target_pairs={{0,2},{2,4},{4,6},{6,8},{8,10},{10,12},{12,14},{14,16},{16,18},{18... | collective-permute-start | bytes 786440 | tf_op jit(solution)/shard_map/ppermute | solution.py:29
  35.6 1.4 fusion.37
  37.8 1.4 fusion.9
  39.4 5.3 %all_to_all.16 = bf16[2,6,128,256]{3,2,1,0:T(8,128)(2,1)S(1)} all-to-all(bf16[2,6,128,256]{3,2,1,0:T(8,128)(2,1)S(1)} %broadcast_in_dim.21), channel_id=1, replica_groups=mesh['fsdp'=128,'dp'=2] {'dp'}, dimensions={0} | all-to-all | bytes 1572864 | tf_op jit(solution)/shard_map/all_to_all | solution.py:34
  44.8 1.4 fusion.144
  46.2 2.8 %fusion.21 = f32[6,256,256]{1,2,0:T(8,128)S(1)} fusion(f32[6,256,256]{2,1,0:T(8,128)S(1)} %copy-done.1, bf16[6,256,256]{2,1,0:T(8,128)(2,1)S(1)} %bitcast.79, f32[6,256,256]{2,1,0:T(8,128)S(1)} %copy-done.2), kind=kOutput, calls=%fused_computation.27 | convolution fusion | flops 1209532416 | bytes 5505024 | tf_op jit(solution)/shard_map/jba,jbd->jad/dot_general | solution.py:59
  49.0 1.6 %fusion.143 = f32[6,256,256]{2,1,0:T(8,128)S(1)} fusion(f32[6,256,256]{1,2,0:T(8,128)S(1)} %fusion.21, f32[6,256,256]{2,1,0:T(8,128)S(1)} %copy-done), kind=kOutput, calls=%fused_computation.177 | convolution fusion | flops 1207959552 | bytes 4718592 | tf_op jit(solution)/shard_map/jad,jde->jae/dot_general | solution.py:57
  50.7 3.6 %broadcast_select_fusion = (f32[6,256,256]{2,1,0:T(8,128)}, f32[6,256,256]{2,1,0:T(8,128)}, f32[6,256,256]{2,1,0:T(8,128)S(1)}) fusion(pred[6]{0:T(512)(128)(4,1)S(1)} %iota_compare_fusion.10, f32[6,256,256]{2,1,0:T(8,128)S(1)} %copy-done.3, bf16[6,2,128,256]{3,2,1,0:T(8,128)(2,1)S(1)} %copy.79, f32[6,256,256]{2,1,0:T(8,128)S(1)} %copy-done.2, ...), kind=kOutput, calls=%fused_computation.29 | convolution fusion | flops 1211891712 | bytes 11796486 | tf_op jit(solution)/shard_map/jad,jde->jae/dot_general | solution.py:51
  54.3 2.7 %fusion.1 = f32[6,256,256]{1,2,0:T(8,128)S(1)} fusion(f32[6,256,256]{2,1,0:T(8,128)S(1)} %copy-done.1, f32[6,256,256]{2,1,0:T(8,128)S(1)} %fusion.143, f32[6,256,256]{2,1,0:T(8,128)S(1)} %get-tuple-element.29, f32[6,256,256]{2,1,0:T(8,128)S(1)} %copy-done.3), kind=kOutput, calls=%fused_computation.2 | convolution fusion | flops 1211105280 | bytes 7864320 | tf_op jit(solution)/shard_map/jab,jbd->jad/dot_general | solution.py:69
  57.0 1.9 %fusion.145 = f32[6,256,256]{2,1,0:T(8,128)S(1)} fusion(f32[6,256,256]{1,2,0:T(8,128)S(1)} %fusion.1, f32[6,256,256]{2,1,0:T(8,128)S(1)} %copy-done), kind=kOutput, calls=%fused_computation.179 | convolution fusion | flops 1207959552 | bytes 4718592 | tf_op jit(solution)/shard_map/jad,jed->jae/dot_general | solution.py:67
  59.0 6.2 %collective-permute-start.5 = (f32[6,128,256]{2,1,0:T(8,128)S(1)}, f32[6,128,256]{2,1,0:T(8,128)S(1)}, u32[]{:S(2)}, u32[]{:S(2)}) collective-permute-start(f32[6,128,256]{2,1,0:T(8,128)S(1)} %dynamic-slice_select_fusion), channel_id=1, source_target_pairs={{0,2},{2,4},{4,6},{6,8},{8,10},{10,12},{12,14},{14,16},{16,18},{18... | collective-permute-start | bytes 2359304 | tf_op jit(solution)/shard_map/ppermute | solution.py:29
  66.5 2.7 %collective-permute-start.7 = (f32[6,128,256]{2,1,0:T(8,128)S(1)}, f32[6,128,256]{2,1,0:T(8,128)S(1)}, u32[]{:S(2)}, u32[]{:S(2)}) collective-permute-start(f32[6,128,256]{2,1,0:T(8,128)S(1)} %dynamic-slice_select_fusion), channel_id=1, source_target_pairs={{4,0},{6,2},{8,4},{10,6},{12,8},{14,10},{16,12},{18,14},{20,16},{2... | collective-permute-start | bytes 2359304 | tf_op jit(solution)/shard_map/ppermute | solution.py:29
  71.1 5.0 %collective-permute-start.4 = (f32[6,128,256]{2,1,0:T(8,128)S(1)}, f32[6,128,256]{2,1,0:T(8,128)S(1)}, u32[]{:S(2)}, u32[]{:S(2)}) collective-permute-start(f32[6,128,256]{2,1,0:T(8,128)S(1)} %dynamic-slice_select_fusion), channel_id=1, source_target_pairs={{0,4},{2,6},{4,8},{6,10},{8,12},{10,14},{12,16},{14,18},{16,20},{1... | collective-permute-start | bytes 2359304 | tf_op jit(solution)/shard_map/ppermute | solution.py:29
  76.0 2.7 %collective-permute-start.6 = (f32[6,128,256]{2,1,0:T(8,128)S(1)}, f32[6,128,256]{2,1,0:T(8,128)S(1)}, u32[]{:S(2)}, u32[]{:S(2)}) collective-permute-start(f32[6,128,256]{2,1,0:T(8,128)S(1)} %dynamic-slice_select_fusion), channel_id=1, source_target_pairs={{2,0},{4,2},{6,4},{8,6},{10,8},{12,10},{14,12},{16,14},{18,16},{20... | collective-permute-start | bytes 2359304 | tf_op jit(solution)/shard_map/ppermute | solution.py:29
  79.8 18.8 %collective-permute-done.5 = f32[6,128,256]{2,1,0:T(8,128)S(1)} collective-permute-done((f32[6,128,256]{2,1,0:T(8,128)S(1)}, f32[6,128,256]{2,1,0:T(8,128)S(1)}, u32[]{:S(2)}, u32[]{:S(2)}) %collective-permute-start.5) | collective-permute-done | bytes 786464 | tf_op jit(solution)/shard_map/ppermute | solution.py:29
  99.6 20.4 %collective-permute-done.7 = f32[6,128,256]{2,1,0:T(8,128)S(1)} collective-permute-done((f32[6,128,256]{2,1,0:T(8,128)S(1)}, f32[6,128,256]{2,1,0:T(8,128)S(1)}, u32[]{:S(2)}, u32[]{:S(2)}) %collective-permute-start.7) | collective-permute-done | bytes 786464 | tf_op jit(solution)/shard_map/ppermute | solution.py:29
  121.0 1.1 fusion.10
  122.1 22.2 %collective-permute-done.6 = f32[6,128,256]{2,1,0:T(8,128)S(1)} collective-permute-done((f32[6,128,256]{2,1,0:T(8,128)S(1)}, f32[6,128,256]{2,1,0:T(8,128)S(1)}, u32[]{:S(2)}, u32[]{:S(2)}) %collective-permute-start.6) | collective-permute-done | bytes 786464 | tf_op jit(solution)/shard_map/ppermute | solution.py:29
  145.6 4.7 %all_to_all.17 = f32[2,4,128,256]{3,2,1,0:T(8,128)S(1)} all-to-all(f32[2,4,128,256]{3,2,1,0:T(8,128)S(1)} %broadcast_in_dim.23), channel_id=1, replica_groups=mesh['fsdp'=128,'dp'=2] {'dp'}, dimensions={0} | all-to-all | bytes 2097152 | tf_op jit(solution)/shard_map/all_to_all | solution.py:34
  (66 shorter events, 25.1 us)
Async XLA Ops:
  0.6 48.4 %copy-start = (f32[6,256,256]{2,1,0:T(8,128)S(1)}, f32[6,256,256]{2,1,0:T(8,128)}, u32[]{:S(2)}) copy-start(f32[6,256,256]{2,1,0:T(8,128)} %param.11) | copy-start | bytes 4718596
  0.6 20.4 %copy-start.5 = (s32[384]{0:T(512)S(1)}, s32[384]{0:T(512)}, u32[]{:S(2)}) copy-start(s32[384]{0:T(512)} %param.13) | copy-start | bytes 4612
  1.9 21.7 %copy-start.4 = (s32[128]{0:T(128)S(1)}, s32[128]{0:T(128)}, u32[]{:S(2)}) copy-start(s32[128]{0:T(128)} %param.12) | copy-start | bytes 1540
  7.4 28.2 %collective-permute-start.1 = (bf16[4,128,256]{2,0,1:T(4,128)(2,1)}, bf16[4,128,256]{2,0,1:T(4,128)(2,1)}, u32[]{:S(2)}, u32[]{:S(2)}) collective-permute-start(bf16[4,128,256]{2,0,1:T(4,128)(2,1)} %copy.73), channel_id=1, source_target_pairs={{2,0},{4,2},{6,4},{8,6},{10,8},{12,10},{14,12},{16,14},{18,16},{20... | collective-permute-start | bytes 786440 | tf_op jit(solution)/shard_map/ppermute | solution.py:29
  12.3 24.6 %collective-permute-start = (bf16[4,128,256]{2,0,1:T(4,128)(2,1)}, bf16[4,128,256]{2,0,1:T(4,128)(2,1)S(1)}, u32[]{:S(2)}, u32[]{:S(2)}) collective-permute-start(bf16[4,128,256]{2,0,1:T(4,128)(2,1)} %copy.73), channel_id=1, source_target_pairs={{4,0},{6,2},{8,4},{10,6},{12,8},{14,10},{16,12},{18,14},{20,16},{2... | collective-permute-start | bytes 786440 | tf_op jit(solution)/shard_map/ppermute | solution.py:29
  14.6 22.8 %collective-permute-start.3 = (bf16[4,128,256]{2,0,1:T(4,128)(2,1)}, bf16[4,128,256]{2,0,1:T(4,128)(2,1)S(1)}, u32[]{:S(2)}, u32[]{:S(2)}) collective-permute-start(bf16[4,128,256]{2,0,1:T(4,128)(2,1)} %copy.73), channel_id=1, source_target_pairs={{0,4},{2,6},{4,8},{6,10},{8,12},{10,14},{12,16},{14,18},{16,20},{1... | collective-permute-start | bytes 786440 | tf_op jit(solution)/shard_map/ppermute | solution.py:29
  19.1 18.7 %collective-permute-start.2 = (bf16[4,128,256]{2,0,1:T(4,128)(2,1)}, bf16[4,128,256]{2,0,1:T(4,128)(2,1)}, u32[]{:S(2)}, u32[]{:S(2)}) collective-permute-start(bf16[4,128,256]{2,0,1:T(4,128)(2,1)} %copy.73), channel_id=1, source_target_pairs={{0,2},{2,4},{4,6},{6,8},{8,10},{10,12},{12,14},{14,16},{16,18},{18... | collective-permute-start | bytes 786440 | tf_op jit(solution)/shard_map/ppermute | solution.py:29
  39.4 5.4 %copy-start.1 = (f32[6,256,256]{2,1,0:T(8,128)S(1)}, f32[6,256,256]{2,1,0:T(8,128)}, u32[]{:S(2)}) copy-start(f32[6,256,256]{2,1,0:T(8,128)} %param.10) | copy-start | bytes 4718596
  44.8 1.5 copy-start.2
  49.0 1.7 %copy-start.3 = (f32[6,256,256]{2,1,0:T(8,128)S(1)}, f32[6,256,256]{2,1,0:T(8,128)}, u32[]{:S(2)}) copy-start(f32[6,256,256]{2,1,0:T(8,128)} %param.9) | copy-start | bytes 4718596
  59.0 39.5 %collective-permute-start.5 = (f32[6,128,256]{2,1,0:T(8,128)S(1)}, f32[6,128,256]{2,1,0:T(8,128)S(1)}, u32[]{:S(2)}, u32[]{:S(2)}) collective-permute-start(f32[6,128,256]{2,1,0:T(8,128)S(1)} %dynamic-slice_select_fusion), channel_id=1, source_target_pairs={{0,2},{2,4},{4,6},{6,8},{8,10},{10,12},{12,14},{14,16},{16,18},{18... | collective-permute-start | bytes 2359304 | tf_op jit(solution)/shard_map/ppermute | solution.py:29
  66.5 53.5 %collective-permute-start.7 = (f32[6,128,256]{2,1,0:T(8,128)S(1)}, f32[6,128,256]{2,1,0:T(8,128)S(1)}, u32[]{:S(2)}, u32[]{:S(2)}) collective-permute-start(f32[6,128,256]{2,1,0:T(8,128)S(1)} %dynamic-slice_select_fusion), channel_id=1, source_target_pairs={{4,0},{6,2},{8,4},{10,6},{12,8},{14,10},{16,12},{18,14},{20,16},{2... | collective-permute-start | bytes 2359304 | tf_op jit(solution)/shard_map/ppermute | solution.py:29
  71.1 49.9 %collective-permute-start.4 = (f32[6,128,256]{2,1,0:T(8,128)S(1)}, f32[6,128,256]{2,1,0:T(8,128)S(1)}, u32[]{:S(2)}, u32[]{:S(2)}) collective-permute-start(f32[6,128,256]{2,1,0:T(8,128)S(1)} %dynamic-slice_select_fusion), channel_id=1, source_target_pairs={{0,4},{2,6},{4,8},{6,10},{8,12},{10,14},{12,16},{14,18},{16,20},{1... | collective-permute-start | bytes 2359304 | tf_op jit(solution)/shard_map/ppermute | solution.py:29
  76.0 68.3 %collective-permute-start.6 = (f32[6,128,256]{2,1,0:T(8,128)S(1)}, f32[6,128,256]{2,1,0:T(8,128)S(1)}, u32[]{:S(2)}, u32[]{:S(2)}) collective-permute-start(f32[6,128,256]{2,1,0:T(8,128)S(1)} %dynamic-slice_select_fusion), channel_id=1, source_target_pairs={{2,0},{4,2},{6,4},{8,6},{10,8},{12,10},{14,12},{16,14},{18,16},{20... | collective-permute-start | bytes 2359304 | tf_op jit(solution)/shard_map/ppermute | solution.py:29
where the time goes:
time: 152 us; the launch traced here: 151 us
  waiting for transfers between devices  61.3 us (40%)
  starting transfers between devices  30.1 us (20%)
  matrix products  23.4 us (15%)
  other arithmetic  15.7 us (10%)
  blocking collectives  14.5 us (10%)
  local copies, waits for them, and re-layouts  5.14 us (3%)
    ppermute x8, waiting for transfers between devices, from_behind(): lax.ppermute(value, axis, [(source, source + steps) for source in range(i...  61.3 us
    ppermute x8, starting transfers between devices, from_behind(): lax.ppermute(value, axis, [(source, source + steps) for source in range(i...  30.1 us
    all_to_all x2, blocking collectives, sent_to_all(): lax.all_to_all(jnp.broadcast_to(x[None], (length, *x.shape)), axis, 0, 0,...  10 us
    dot_general x5, matrix products, body(): jnp.einsum('js,jab->sab', matching.astype(jnp.float32), arriving, precisi...  5.33 us
    all_to_all x1, blocking collectives, summed_on_arrival(): lax.all_to_all(blocks, axis, split_axis=0, concat_axis=0, tiled=True)  4.46 us
    dot_general x5, matrix products, body(): jnp.einsum('js,sab->jab', matching.astype(jnp.bfloat16), arriving, prefer...  3.99 us
    lt x6, other arithmetic, linking(): jnp.arange(slot_count)[None, :] < hold_count  3.77 us
    add x6, other arithmetic, linking(): holder_pos = hold_start + jnp.arange(slot_count, dtype=jnp.int32)  3.68 us
  transfers between devices with their start and end apart: 8, of which 3 were waited for; matrix products, arithmetic and copies ran while one was open for 16% of the time, Pallas kernels for 0%

commit v1 on v0

v1 whole, which is shorter than its diff:
```python
import functools

import jax
import jax.numpy as jnp
from jax import lax
from jax.experimental import pallas as pl
from jax.experimental.pallas import tpu as pltpu
from jax.sharding import PartitionSpec as P

STEP = 10
BETA_ONE = 0.9
BETA_TWO = 0.95
EPSILON = 1e-08
TOP = 32766.0
MESH = pl.DeviceIdType.MESH
F32 = jnp.float32
BF16 = jnp.bfloat16
I16 = jnp.int16


def neighbours(devices):
    me = lax.axis_index("fsdp")
    core = lax.axis_index("dp")
    right = {"fsdp": lax.rem(me + 1, devices)}
    left = {"fsdp": lax.rem(me + devices - 1, devices)}
    twin = {"dp": 1 - core}
    return core, right, left, twin


def greet(peers):
    barrier = pltpu.get_barrier_semaphore()
    for peer in peers:
        pl.semaphore_signal(barrier, inc=1, device_id=peer, device_id_type=MESH)
    pl.semaphore_wait(barrier, len(peers))


def push(src, dst, send_sem, recv_sem, peer):
    return pltpu.make_async_remote_copy(
        src_ref=src,
        dst_ref=dst,
        send_sem=send_sem,
        recv_sem=recv_sem,
        device_id=peer,
        device_id_type=MESH,
    )


def gather_kernel(devices, grad, out, mine, theirs, other, load_sem, twin_sem, ring_send, ring_recv, hand_send, hand_recv):
    core, right, left, twin = neighbours(devices)
    slots = grad.shape[1]
    half = grad.shape[2] // 2
    rows = pl.ds(pl.multiple_of(core * half, half), half)
    other_rows = pl.ds(pl.multiple_of((1 - core) * half, half), half)
    load_other = pltpu.make_async_copy(grad.at[0, :, other_rows], other, load_sem.at[0])
    load_mine = pltpu.make_async_copy(grad.at[0, :, rows], mine, load_sem.at[1])
    load_other.start()
    load_mine.start()
    greet((twin, right, left))
    load_other.wait()
    swap = push(other, theirs, twin_sem.at[0], twin_sem.at[1], twin)
    swap.start()
    load_mine.wait()
    swap.wait_recv()
    for s in range(slots):
        out[2, s, rows] = (mine[s].astype(F32) + theirs[s].astype(F32)).astype(BF16)

    def part(k, s):
        return out.at[k, s, rows]

    def ring(src_k, dst_k, s, peer):
        return push(part(src_k, s), part(dst_k, s), ring_send.at[dst_k, s], ring_recv.at[dst_k, s], peer)

    def hand(k, s):
        return push(part(k, s), part(k, s), hand_send.at[k, s], hand_recv.at[k, s], twin)

    copies = []
    for s in range(slots):
        for copy in (ring(2, 1, s, right), ring(2, 3, s, left), hand(2, s)):
            copy.start()
            copies.append(copy)
    relays = []
    for s in range(slots):
        for near, far, peer in ((1, 0, right), (3, 4, left)):
            ring(2, near, s, peer).wait_recv()
            relay = ring(near, far, s, peer)
            relay.start()
            pass_on = hand(near, s)
            pass_on.start()
            copies += [relay, pass_on]
            relays.append((far, s, relay))
    for far, s, relay in relays:
        relay.wait_recv()
        pass_on = hand(far, s)
        pass_on.start()
        copies.append(pass_on)
    swap.wait_send()
    for copy in copies:
        copy.wait_send()
    for k in range(5):
        for s in range(slots):
            hand(k, s).wait_recv()


def split(x):
    high = x.astype(BF16)
    return high, (x - high.astype(F32)).astype(BF16)


def dot(a, b, dims):
    return lax.dot_general(a, b, (dims, ((), ())), preferred_element_type=F32)


def dot_three(a, b, dims):
    return dot(a[0], b[0], dims) + (dot(a[0], b[1], dims) + dot(a[1], b[0], dims))


NN = ((1,), (0,))
TN = ((0,), (0,))
NT = ((1,), (1,))


def step_kernel(devices, starts, owners, gathered, moment, second, left, right, first_out, second_out, codes, scales, table):
    j = pl.program_id(0)
    me = lax.axis_index("fsdp")
    core = lax.axis_index("dp")
    blocks = owners.shape[0]
    slots = gathered.shape[0] // 5
    half = left.shape[1] // 2

    def start_of(device):
        value = starts[jnp.clip(device, 0, devices - 1)]
        return jnp.where(device < 0, -1, jnp.where(device >= devices, blocks, value))

    @pl.when(j == 0)
    def _():
        codes[...] = jnp.zeros(codes.shape, codes.dtype)
        scales[...] = jnp.zeros(scales.shape, scales.dtype)
        base = jnp.maximum(start_of(me - 2), 0)
        below = jnp.int32(0)
        for k in range(5 * slots):
            at = base + k
            owner = owners[jnp.minimum(at, blocks - 1)]
            below += jnp.where((at < blocks) & (owner < me), 1, 0)
        table[0] = base + below

    block = table[0] + j
    safe = jnp.minimum(block, blocks - 1)
    live = (block < blocks) & (owners[safe] == me)
    place = jnp.int32(0)
    for delta in (-1, 0, 1, 2):
        place += jnp.where(start_of(me + delta) <= block, 1, 0)
    slot = block - starts[jnp.clip(me + place - 2, 0, devices - 1)]
    index = jnp.where(live, place * slots + slot, 0)

    gradient = gathered[index]
    l_two, r_two = split(left[0]), split(right[0])
    moment_new = BETA_ONE * moment[0] + (1.0 - BETA_ONE) * gradient.astype(F32)
    first_out[0] = jnp.where(live, moment_new, 0.0)
    half_turned = dot(l_two[0], gradient, TN) + dot(l_two[1], gradient, TN)
    turned = dot_three(split(half_turned), r_two, NN)
    turned_moment = dot_three(split(dot_three(l_two, split(moment_new), TN)), r_two, NN)
    second_next = BETA_TWO * second[0] + (1.0 - BETA_TWO) * turned * turned
    second_out[0] = jnp.where(live, second_next, 0.0)
    bias_one = 1.0 - BETA_ONE**STEP
    bias_two = 1.0 - BETA_TWO**STEP
    scaled = turned_moment / bias_one / (jnp.sqrt(second_next / bias_two) + EPSILON)
    l_half = split(left[0, pl.ds(pl.multiple_of(core * half, half), half)])
    update = dot_three(split(dot_three(l_half, split(scaled), NN)), r_two, NT)
    largest = jnp.maximum(jnp.max(jnp.abs(update), axis=0, keepdims=True), 1e-30)
    code = jnp.round(update * (TOP / largest)).astype(jnp.int32)

    @pl.when(live)
    def _():
        codes[index] = code.astype(I16)
        scales[index, 0:1] = largest * (1.0 / TOP)


def return_kernel(
    devices, codes, scales, out, out_scales, far_in, far_scales, merged, merged_scales, far_send, far_recv, ring_send, ring_recv, hand_send, hand_recv,
    sf_send, sf_recv, sr_send, sr_recv, sh_send, sh_recv
):
    core, right, left, twin = neighbours(devices)
    slots = codes.shape[1]
    half = codes.shape[2]
    rows = pl.ds(pl.multiple_of(core * half, half), half)
    greet((twin, right, left))
    copies = []
    far = []
    for k, side, peer in ((4, 0, right), (0, 1, left)):
        copy = push(scales.at[k], far_scales.at[side], sf_send.at[side], sf_recv.at[side], peer)
        copy.start()
        far.append(copy)
    far_copies = {}
    for s in range(slots):
        for k, side, peer in ((4, 0, right), (0, 1, left)):
            copy = push(codes.at[k, s], far_in.at[side, s], far_send.at[side, s], far_recv.at[side, s], peer)
            copy.start()
            far_copies[side, s] = copy

    def hand(k, s):
        return push(out.at[k, s, rows], out.at[k, s, rows], hand_send.at[k, s], hand_recv.at[k, s], twin)

    def hand_scales(k):
        return push(out_scales.at[k, core], out_scales.at[k, core], sh_send.at[k], sh_recv.at[k], twin)

    out_scales[2, core] = scales[2]
    for s in range(slots):
        out[2, s, rows] = codes[2, s]
    copy = hand_scales(2)
    copy.start()
    copies.append(copy)
    for s in range(slots):
        copy = hand(2, s)
        copy.start()
        copies.append(copy)

    near_scales = []
    for k, side, peer in ((3, 0, right), (1, 1, left)):
        far[side].wait_recv()
        merged_scales[side] = scales[k] + far_scales[side]
        copy = push(merged_scales.at[side], out_scales.at[side, core], sr_send.at[side], sr_recv.at[side], peer)
        copy.start()
        near_scales.append(copy)
    near = []
    for s in range(slots):
        for k, side, peer in ((3, 0, right), (1, 1, left)):
            far_copies[side, s].wait_recv()
            merged[side, s] = codes[k, s] + far_in[side, s]
            copy = push(merged.at[side, s], out.at[side, s, rows], ring_send.at[side, s], ring_recv.at[side, s], peer)
            copy.start()
            near.append((side, s, copy))
    for side in range(2):
        near_scales[side].wait_recv()
        copy = hand_scales(side)
        copy.start()
        copies.append(copy)
    for side, s, ring in near:
        ring.wait_recv()
        copy = hand(side, s)
        copy.start()
        copies.append(copy)
    for copy in copies + far + near_scales + list(far_copies.values()) + [ring for _, _, ring in near]:
        copy.wait_send()
    for k in range(3):
        hand_scales(k).wait_recv()
        for s in range(slots):
            hand(k, s).wait_recv()


def decode_kernel(codes, scales, out):
    s = pl.program_id(0)
    half = out.shape[1] // 2
    for core in range(2):
        rows = pl.ds(core * half, half)
        total = 0.0
        for k in range(3):
            total += codes[k, s, rows].astype(jnp.int32).astype(F32) * scales[k, core, pl.ds(s, 1)]
        out[0, rows] = total


def body(gradients, first_moment, second_moment, left_basis, right_basis, shard_starts, block_owners):
    devices = lax.axis_size("fsdp")
    slots = gradients.shape[1]
    owned, width = first_moment.shape[0], first_moment.shape[1]
    half = width // 2
    any_space = pl.BlockSpec(memory_space=pl.ANY)
    in_vmem = pl.BlockSpec(memory_space=pltpu.VMEM)
    dma = pltpu.SemaphoreType.DMA
    gathered = pl.pallas_call(
        functools.partial(gather_kernel, devices),
        out_shape=pltpu.VMEM((5, slots, width, width), BF16),
        in_specs=[any_space],
        out_specs=in_vmem,
        scratch_shapes=[pltpu.VMEM((slots, half, width), BF16)] * 3
        + [dma((2,)), dma((2,)), dma((5, slots)), dma((5, slots)), dma((5, slots)), dma((5, slots))],
        compiler_params=pltpu.CompilerParams(collective_id=0, has_side_effects=True),
        name="gather",
    )(gradients)

    block = pl.BlockSpec((1, width, width), lambda j, *_: (j, 0, 0))
    first_new, second_new, codes, scales = pl.pallas_call(
        functools.partial(step_kernel, devices),
        grid_spec=pltpu.PrefetchScalarGridSpec(
            num_scalar_prefetch=2,
            grid=(owned,),
            in_specs=[in_vmem, block, block, block, block],
            out_specs=[block, block, in_vmem, in_vmem],
            scratch_shapes=[pltpu.SMEM((1,), jnp.int32)],
        ),
        out_shape=[
            jax.ShapeDtypeStruct(first_moment.shape, F32),
            jax.ShapeDtypeStruct(first_moment.shape, F32),
            pltpu.VMEM((5 * slots, half, width), I16),
            pltpu.VMEM((5 * slots, 1, width), F32),
        ],
        name="step",
    )(shard_starts, block_owners, gathered.reshape(5 * slots, width, width), first_moment, second_moment, left_basis, right_basis)

    out, out_scales = pl.pallas_call(
        functools.partial(return_kernel, devices),
        out_shape=[
            pltpu.VMEM((3, slots, width, width), I16),
            pltpu.VMEM((3, 2, slots, width), F32),
        ],
        in_specs=[in_vmem, in_vmem],
        out_specs=[in_vmem, in_vmem],
        scratch_shapes=[
            pltpu.VMEM((2, slots, half, width), I16),
            pltpu.VMEM((2, slots, width), F32),
            pltpu.VMEM((2, slots, half, width), I16),
            pltpu.VMEM((2, slots, width), F32),
            dma((2, slots)), dma((2, slots)), dma((2, slots)), dma((2, slots)), dma((3, slots)), dma((3, slots)),
            dma((2,)), dma((2,)), dma((2,)), dma((2,)), dma((3,)), dma((3,)),
        ],
        compiler_params=pltpu.CompilerParams(collective_id=1, has_side_effects=True),
        name="bring",
    )(codes.reshape(5, slots, half, width), scales.reshape(5, slots, width))

    direction = pl.pallas_call(
        decode_kernel,
        grid=(slots,),
        out_shape=jax.ShapeDtypeStruct((slots, width, width), F32),
        in_specs=[in_vmem, in_vmem],
        out_specs=pl.BlockSpec((1, width, width), lambda s: (s, 0, 0)),
        name="decode",
    )(out, out_scales)
    return direction, first_new, second_new


def solution(mesh):
    in_specs = (
        P("dp", "fsdp", None, None),
        P("fsdp", None, None),
        P("fsdp", None, None),
        P("fsdp", None, None),
        P("fsdp", None, None),
        P(),
        P(),
    )
    out_specs = (P("fsdp", None, None), P("fsdp", None, None), P("fsdp", None, None))
    return jax.shard_map(body, mesh=mesh, in_specs=in_specs, out_specs=out_specs, check_vma=False)
```

time: 152 us -> 74.8 us (0.49)
  the two profiles are of different devices: /device:TPU:103 before, /device:TPU:1 now
where the time goes in v1:
time: 74.8 us; the launch traced here: 74.6 us
  Pallas kernels  69 us (92%)
  local copies, waits for them, and re-layouts  4.93 us (7%)
    pallas_call x1, Pallas kernels, body(): pl.pallas_call(functools.partial(gather_kernel, devices), out_shape=pltpu...  30.2 us
    pallas_call x1, Pallas kernels, body(): pl.pallas_call(functools.partial(return_kernel, devices), out_shape=[pltp...  22.7 us
    pallas_call x1, Pallas kernels, body(): pl.pallas_call(functools.partial(step_kernel, devices), grid_spec=pltpu.P...  12.9 us
    unnamed x8, local copies, waits for them, and re-layouts  4.31 us
    pallas_call x1, Pallas kernels, body(): pl.pallas_call(decode_kernel, grid=(slots,), out_shape=jax.ShapeDtypeStru...  3.12 us

profile of v1, /device:TPU:1, one launch (start us, length us, event | category | flops | bytes accessed | tf_op | source)
XLA Modules:
  0.0 74.6 jit_solution(12109762689983077803)
XLA Ops:
  0.6 30.2 %gather.1 = bf16[5,4,256,256]{3,2,1,0:T(8,128)(2,1)S(1)} custom-call(bf16[1,4,256,256]{3,2,1,0:T(8,128)(2,1)} %grad.1), custom_call_target="tpu_custom_call" | custom-call | tf_op jit(solution)/shard_map/gather/pallas_call | solution.py:269
  30.9 0.0 copy-start
  30.9 1.5 %copy-done = bf16[5,4,256,256]{3,2,1,0:T(8,128)(2,1)} copy-done((bf16[5,4,256,256]{3,2,1,0:T(8,128)(2,1)}, bf16[5,4,256,256]{3,2,1,0:T(8,128)(2,1)S(1)}, u32[]{:S(2)}) %copy-start) | copy-done | bytes 2621464
  32.4 12.9 %step.1 = (f32[6,256,256]{2,1,0:T(8,128)}, f32[6,256,256]{2,1,0:T(8,128)}, s16[20,128,256]{2,1,0:T(8,128)(2,1)S(1)}, f32[20,1,256]{2,1,0:T(1,128)S(1)}) custom-call(s32[128]{0:T(128)} %starts.1, s32[384]{0:T(512)} %owners.1, bf16[20,256,256]{2,1,0:T(8,128)(2,1)} %bitcast.2, f32[6,256,256]{2,1,0:T(8,128)} %moment.1, f32[6,256,256]{2,1,0:T(8,128)} %second.1, ...), custom_call_target="tpu_custom_call" | custom-call | tf_op jit(solution)/shard_map/step/pallas_call | solution.py:281
  45.3 0.0 copy-start.2
  45.3 1.1 %copy-done.2 = s16[20,128,256]{2,1,0:T(8,128)(2,1)} copy-done((s16[20,128,256]{2,1,0:T(8,128)(2,1)}, s16[20,128,256]{2,1,0:T(8,128)(2,1)S(1)}, u32[]{:S(2)}) %copy-start.2) | copy-done | bytes 1310744
  46.4 0.6 reshape.17.scales
  47.0 22.7 %bring.1 = (s16[3,4,256,256]{3,2,1,0:T(8,128)(2,1)S(1)}, f32[3,2,4,256]{3,2,1,0:T(4,128)S(1)}) custom-call(s16[5,4,128,256]{3,2,1,0:T(8,128)(2,1)} %bitcast.3, f32[5,4,256]{2,1,0:T(4,128)} %reshape.17.scales), custom_call_target="tpu_custom_call" | custom-call | tf_op jit(solution)/shard_map/bring/pallas_call | solution.py:299
  69.7 0.0 copy-start.1
  69.7 1.2 %copy-done.1 = s16[3,4,256,256]{3,2,1,0:T(8,128)(2,1)} copy-done((s16[3,4,256,256]{3,2,1,0:T(8,128)(2,1)}, s16[3,4,256,256]{3,2,1,0:T(8,128)(2,1)S(1)}, u32[]{:S(2)}) %copy-start.1) | copy-done | bytes 1572888
  70.9 0.0 copy-start.3
  70.9 0.6 copy-done.3
  71.5 3.1 %decode.1 = f32[4,256,256]{2,1,0:T(8,128)} custom-call(s16[3,4,256,256]{3,2,1,0:T(8,128)(2,1)} %copy-done.1, f32[3,2,4,256]{3,2,1,0:T(4,128)} %copy-done.3), custom_call_target="tpu_custom_call" | custom-call | tf_op jit(solution)/shard_map/decode/pallas_call | solution.py:319
  (1 shorter events, 0.0 us)
Async XLA Ops:
  30.9 1.5 %copy-start = (bf16[5,4,256,256]{3,2,1,0:T(8,128)(2,1)}, bf16[5,4,256,256]{3,2,1,0:T(8,128)(2,1)S(1)}, u32[]{:S(2)}) copy-start(bf16[5,4,256,256]{3,2,1,0:T(8,128)(2,1)S(1)} %gather.1) | copy-start | bytes 7864324
  45.3 1.1 %copy-start.2 = (s16[20,128,256]{2,1,0:T(8,128)(2,1)}, s16[20,128,256]{2,1,0:T(8,128)(2,1)S(1)}, u32[]{:S(2)}) copy-start(s16[20,128,256]{2,1,0:T(8,128)(2,1)S(1)} %get-tuple-element.9) | copy-start | bytes 3932164
  69.7 1.2 %copy-start.1 = (s16[3,4,256,256]{3,2,1,0:T(8,128)(2,1)}, s16[3,4,256,256]{3,2,1,0:T(8,128)(2,1)S(1)}, u32[]{:S(2)}) copy-start(s16[3,4,256,256]{3,2,1,0:T(8,128)(2,1)S(1)} %get-tuple-element.11.codes) | copy-start | bytes 4718596
  70.9 0.6 copy-start.3

commit v2 on v1

v2 whole, which is shorter than its diff:
```python
import functools

import jax
import jax.numpy as jnp
from jax import lax
from jax.experimental import pallas as pl
from jax.experimental.pallas import tpu as pltpu
from jax.sharding import PartitionSpec as P

STEP = 10
BETA_ONE = 0.9
BETA_TWO = 0.95
EPSILON = 1e-08
TOP = 32766.0
ROOM = 24 * 2**20
MESH = pl.DeviceIdType.MESH
F32 = jnp.float32
BF16 = jnp.bfloat16
I16 = jnp.int16


def neighbours(devices):
    me = lax.axis_index("fsdp")
    core = lax.axis_index("dp")
    right = {"fsdp": jnp.minimum(me + 1, devices - 1)}
    left = {"fsdp": jnp.maximum(me - 1, 0)}
    twin = {"dp": 1 - core}
    return me, core, right, left, twin


def greet(me, devices, right, left, twin):
    barrier = pltpu.get_barrier_semaphore()

    def signal(peer):
        pl.semaphore_signal(barrier, inc=1, device_id=peer, device_id_type=MESH)

    signal(twin)
    pl.when(me < devices - 1)(lambda: signal(right))
    pl.when(me > 0)(lambda: signal(left))
    at_end = (me == 0) | (me == devices - 1)
    pl.when(at_end)(lambda: pl.semaphore_wait(barrier, 2))
    pl.when(~at_end)(lambda: pl.semaphore_wait(barrier, 3))


def push(src, dst, send_sem, recv_sem, peer):
    return pltpu.make_async_remote_copy(
        src_ref=src,
        dst_ref=dst,
        send_sem=send_sem,
        recv_sem=recv_sem,
        device_id=peer,
        device_id_type=MESH,
    )


def gather_kernel(devices, grad, out, mine, theirs, other, load_sem, twin_sem, ring_send, ring_recv, hand_send, hand_recv):
    me, core, right, left, twin = neighbours(devices)
    slots = grad.shape[1]
    half = grad.shape[2] // 2
    rows = pl.ds(pl.multiple_of(core * half, half), half)
    other_rows = pl.ds(pl.multiple_of((1 - core) * half, half), half)
    load_other = pltpu.make_async_copy(grad.at[0, :, other_rows], other, load_sem.at[0])
    load_mine = pltpu.make_async_copy(grad.at[0, :, rows], mine, load_sem.at[1])
    load_other.start()
    load_mine.start()
    greet(me, devices, right, left, twin)
    load_other.wait()
    swap = push(other, theirs, twin_sem.at[0], twin_sem.at[1], twin)
    swap.start()
    load_mine.wait()
    swap.wait_recv()
    for s in range(slots):
        out[2, s, rows] = (mine[s].astype(F32) + theirs[s].astype(F32)).astype(BF16)

    def part(k, s):
        return out.at[k, s, rows]

    def ring(src_k, dst_k, s, peer):
        return push(part(src_k, s), part(dst_k, s), ring_send.at[dst_k, s], ring_recv.at[dst_k, s], peer)

    def hand(k, s):
        return push(part(k, s), part(k, s), hand_send.at[k, s], hand_recv.at[k, s], twin)

    sides = (
        dict(near=1, far=0, peer=right, has=me >= 1, gives=me >= 2, sends=me < devices - 1),
        dict(near=3, far=4, peer=left, has=me < devices - 1, gives=me < devices - 2, sends=me >= 1),
    )

    for side in sides:

        @pl.when(side["sends"])
        def _():
            for s in range(slots):
                ring(2, side["near"], s, side["peer"]).start()

    for s in range(slots):
        hand(2, s).start()
    for s in range(slots):
        for side in sides:

            @pl.when(side["has"])
            def _():
                ring(2, side["near"], s, side["peer"]).wait_recv()

            @pl.when(side["has"] & side["sends"])
            def _():
                ring(side["near"], side["far"], s, side["peer"]).start()

            @pl.when(side["has"])
            def _():
                hand(side["near"], s).start()

    for s in range(slots):
        for side in sides:

            @pl.when(side["gives"])
            def _():
                ring(side["near"], side["far"], s, side["peer"]).wait_recv()
                hand(side["far"], s).start()

    swap.wait_send()
    for s in range(slots):
        hand(2, s).wait_send()
        hand(2, s).wait_recv()
    for side in sides:

        @pl.when(side["sends"])
        def _():
            for s in range(slots):
                ring(2, side["near"], s, side["peer"]).wait_send()

        @pl.when(side["has"] & side["sends"])
        def _():
            for s in range(slots):
                ring(side["near"], side["far"], s, side["peer"]).wait_send()

        @pl.when(side["has"])
        def _():
            for s in range(slots):
                hand(side["near"], s).wait_send()
                hand(side["near"], s).wait_recv()

        @pl.when(side["gives"])
        def _():
            for s in range(slots):
                hand(side["far"], s).wait_send()
                hand(side["far"], s).wait_recv()


def split(x):
    high = x.astype(BF16)
    return high, (x - high.astype(F32)).astype(BF16)


def dot(a, b, dims):
    return lax.dot_general(a, b, (dims, ((), ())), preferred_element_type=F32)


def dot_three(a, b, dims):
    return dot(a[0], b[0], dims) + (dot(a[0], b[1], dims) + dot(a[1], b[0], dims))


NN = ((1,), (0,))
TN = ((0,), (0,))
NT = ((1,), (1,))


GROUP = 2


def step_kernel(devices, starts, owners, gathered, moment, second, left, right, first_out, second_out, codes, scales, table):
    step = pl.program_id(0)
    me = lax.axis_index("fsdp")
    core = lax.axis_index("dp")
    blocks = owners.shape[0]
    slots = gathered.shape[1]
    half = left.shape[1] // 2

    def start_of(device):
        value = starts[jnp.clip(device, 0, devices - 1)]
        return jnp.where(device < 0, -1, jnp.where(device >= devices, blocks, value))

    @pl.when(step == 0)
    def _():
        codes[...] = jnp.zeros(codes.shape, codes.dtype)
        scales[...] = jnp.zeros(scales.shape, scales.dtype)
        base = jnp.maximum(start_of(me - 2), 0)
        below = jnp.int32(0)
        for k in range(5 * slots):
            at = base + k
            owner = owners[jnp.minimum(at, blocks - 1)]
            below += jnp.where((at < blocks) & (owner < me), 1, 0)
        table[0] = base + below

    def solve(at):
        block = table[0] + step * GROUP + at
        safe = jnp.minimum(block, blocks - 1)
        live = (block < blocks) & (owners[safe] == me)
        place = jnp.int32(0)
        for delta in (-1, 0, 1, 2):
            place += jnp.where(start_of(me + delta) <= block, 1, 0)
        slot = block - starts[jnp.clip(me + place - 2, 0, devices - 1)]
        place = jnp.where(live, place, 0)
        slot = jnp.where(live, slot, 0)

        gradient = gathered[place, slot]
        l_two, r_two = split(left[at]), split(right[at])
        moment_new = BETA_ONE * moment[at] + (1.0 - BETA_ONE) * gradient.astype(F32)
        first_out[at] = jnp.where(live, moment_new, 0.0)
        half_turned = dot(l_two[0], gradient, TN) + dot(l_two[1], gradient, TN)
        turned = dot_three(split(half_turned), r_two, NN)
        turned_moment = dot_three(split(dot_three(l_two, split(moment_new), TN)), r_two, NN)
        second_next = BETA_TWO * second[at] + (1.0 - BETA_TWO) * turned * turned
        second_out[at] = jnp.where(live, second_next, 0.0)
        bias_one = 1.0 - BETA_ONE**STEP
        bias_two = 1.0 - BETA_TWO**STEP
        scaled = turned_moment * (1.0 / bias_one) / (jnp.sqrt(second_next * (1.0 / bias_two)) + EPSILON)
        l_half = split(left[at, pl.ds(pl.multiple_of(core * half, half), half)])
        update = dot_three(split(dot_three(l_half, split(scaled), NN)), r_two, NT)
        largest = jnp.maximum(jnp.max(jnp.abs(update), axis=0, keepdims=True), 1e-30)
        code = jnp.round(update * (TOP / largest)).astype(jnp.int32).astype(I16)
        return live, place, slot, code, largest * (1.0 / TOP)

    for live, place, slot, code, scale in [solve(at) for at in range(GROUP)]:

        @pl.when(live)
        def _():
            codes[place, slot] = code
            scales[place, pl.ds(slot, 1)] = scale


def return_kernel(
    devices, codes, scales, out, out_scales, far_in, far_scales, merged, merged_scales, far_send, far_recv, ring_send, ring_recv, hand_send, hand_recv,
    sf_send, sf_recv, sr_send, sr_recv, sh_send, sh_recv
):
    me, core, right, left, twin = neighbours(devices)
    slots = codes.shape[1]
    half = codes.shape[2]
    rows = pl.ds(pl.multiple_of(core * half, half), half)
    greet(me, devices, right, left, twin)

    def hand(k, s):
        return push(out.at[k, s, rows], out.at[k, s, rows], hand_send.at[k, s], hand_recv.at[k, s], twin)

    def hand_scales(k):
        return push(out_scales.at[k, core], out_scales.at[k, core], sh_send.at[k], sh_recv.at[k], twin)

    def far(side, s):
        return push(codes.at[side["far"], s], far_in.at[side["at"], s], far_send.at[side["at"], s], far_recv.at[side["at"], s], side["peer"])

    def far_scale(side):
        return push(scales.at[side["far"]], far_scales.at[side["at"]], sf_send.at[side["at"]], sf_recv.at[side["at"]], side["peer"])

    def ring(side, s):
        return push(
            merged.at[side["at"], s], out.at[side["at"], s, rows], ring_send.at[side["at"], s], ring_recv.at[side["at"], s], side["peer"]
        )

    def ring_scale(side):
        return push(merged_scales.at[side["at"]], out_scales.at[side["at"], core], sr_send.at[side["at"]], sr_recv.at[side["at"]], side["peer"])

    sides = (
        dict(at=0, far=4, near=3, peer=right, has=me >= 1, sends=me < devices - 1),
        dict(at=1, far=0, near=1, peer=left, has=me < devices - 1, sends=me >= 1),
    )
    for side in sides:

        @pl.when(side["sends"])
        def _():
            far_scale(side).start()
            for s in range(slots):
                far(side, s).start()

        @pl.when(~side["has"])
        def _():
            far_in[side["at"]] = jnp.zeros(far_in.shape[1:], I16)
            far_scales[side["at"]] = jnp.zeros(far_scales.shape[1:], F32)
            out[side["at"]] = jnp.zeros(out.shape[1:], I16)
            out_scales[side["at"]] = jnp.zeros(out_scales.shape[1:], F32)

    out_scales[2, core] = scales[2]
    for s in range(slots):
        out[2, s, rows] = codes[2, s]
    hand_scales(2).start()
    for s in range(slots):
        hand(2, s).start()

    for side in sides:

        @pl.when(side["has"])
        def _():
            far_scale(side).wait_recv()

        merged_scales[side["at"]] = scales[side["near"]] + far_scales[side["at"]]

        @pl.when(side["sends"])
        def _():
            ring_scale(side).start()

    for s in range(slots):
        for side in sides:

            @pl.when(side["has"])
            def _():
                far(side, s).wait_recv()

            merged[side["at"], s] = codes[side["near"], s] + far_in[side["at"], s]

            @pl.when(side["sends"])
            def _():
                ring(side, s).start()

    for side in sides:

        @pl.when(side["has"])
        def _():
            ring_scale(side).wait_recv()
            hand_scales(side["at"]).start()

    for s in range(slots):
        for side in sides:

            @pl.when(side["has"])
            def _():
                ring(side, s).wait_recv()
                hand(side["at"], s).start()

    hand_scales(2).wait_send()
    hand_scales(2).wait_recv()
    for s in range(slots):
        hand(2, s).wait_send()
        hand(2, s).wait_recv()
    for side in sides:

        @pl.when(side["sends"])
        def _():
            far_scale(side).wait_send()
            ring_scale(side).wait_send()
            for s in range(slots):
                far(side, s).wait_send()
                ring(side, s).wait_send()

        @pl.when(side["has"])
        def _():
            hand_scales(side["at"]).wait_send()
            hand_scales(side["at"]).wait_recv()
            for s in range(slots):
                hand(side["at"], s).wait_send()
                hand(side["at"], s).wait_recv()


def decode_kernel(codes, scales, out):
    s = pl.program_id(0)
    half = out.shape[1] // 2
    for core in range(2):
        rows = pl.ds(core * half, half)
        total = 0.0
        for k in range(3):
            total += codes[k, s, rows].astype(jnp.int32).astype(F32) * scales[k, core, pl.ds(s, 1)]
        out[0, rows] = total


def body(gradients, first_moment, second_moment, left_basis, right_basis, shard_starts, block_owners):
    devices = lax.axis_size("fsdp")
    slots = gradients.shape[1]
    owned, width = first_moment.shape[0], first_moment.shape[1]
    half = width // 2
    any_space = pl.BlockSpec(memory_space=pl.ANY)
    in_vmem = pl.BlockSpec(memory_space=pltpu.VMEM)
    dma = pltpu.SemaphoreType.DMA
    stay = functools.partial(pltpu.with_memory_space_constraint, memory_space=pltpu.HBM)
    gathered = pl.pallas_call(
        functools.partial(gather_kernel, devices),
        out_shape=pltpu.VMEM((5, slots, width, width), BF16),
        in_specs=[any_space],
        out_specs=in_vmem,
        scratch_shapes=[pltpu.VMEM((slots, half, width), BF16)] * 3
        + [dma((2,)), dma((2,)), dma((5, slots)), dma((5, slots)), dma((5, slots)), dma((5, slots))],
        compiler_params=pltpu.CompilerParams(collective_id=0, has_side_effects=True, vmem_limit_bytes=ROOM),
        name="gather",
    )(stay(gradients))

    keep = functools.partial(pltpu.with_memory_space_constraint, memory_space=pltpu.VMEM)
    block = pl.BlockSpec((GROUP, width, width), lambda j, *_: (j, 0, 0))
    first_new, second_new, codes, scales = pl.pallas_call(
        functools.partial(step_kernel, devices),
        grid_spec=pltpu.PrefetchScalarGridSpec(
            num_scalar_prefetch=2,
            grid=(owned // GROUP,),
            in_specs=[in_vmem, block, block, block, block],
            out_specs=[block, block, in_vmem, in_vmem],
            scratch_shapes=[pltpu.SMEM((1,), jnp.int32)],
        ),
        out_shape=[
            jax.ShapeDtypeStruct(first_moment.shape, F32),
            jax.ShapeDtypeStruct(first_moment.shape, F32),
            pltpu.VMEM((5, slots, half, width), I16),
            pltpu.VMEM((5, slots, width), F32),
        ],
        compiler_params=pltpu.CompilerParams(vmem_limit_bytes=ROOM),
        name="step",
    )(shard_starts, block_owners, keep(gathered), *map(stay, (first_moment, second_moment, left_basis, right_basis)))

    out, out_scales = pl.pallas_call(
        functools.partial(return_kernel, devices),
        out_shape=[
            pltpu.VMEM((3, slots, width, width), I16),
            pltpu.VMEM((3, 2, slots, width), F32),
        ],
        in_specs=[in_vmem, in_vmem],
        out_specs=[in_vmem, in_vmem],
        scratch_shapes=[
            pltpu.VMEM((2, slots, half, width), I16),
            pltpu.VMEM((2, slots, width), F32),
            pltpu.VMEM((2, slots, half, width), I16),
            pltpu.VMEM((2, slots, width), F32),
            dma((2, slots)), dma((2, slots)), dma((2, slots)), dma((2, slots)), dma((3, slots)), dma((3, slots)),
            dma((2,)), dma((2,)), dma((2,)), dma((2,)), dma((3,)), dma((3,)),
        ],
        compiler_params=pltpu.CompilerParams(collective_id=1, has_side_effects=True, vmem_limit_bytes=ROOM),
        name="bring",
    )(keep(codes), keep(scales))

    direction = pl.pallas_call(
        decode_kernel,
        grid=(slots,),
        out_shape=jax.ShapeDtypeStruct((slots, width, width), F32),
        in_specs=[in_vmem, in_vmem],
        out_specs=pl.BlockSpec((1, width, width), lambda s: (s, 0, 0)),
        compiler_params=pltpu.CompilerParams(vmem_limit_bytes=ROOM),
        name="decode",
    )(keep(out), keep(out_scales))
    return direction, first_new, second_new


def solution(mesh):
    in_specs = (
        P("dp", "fsdp", None, None),
        P("fsdp", None, None),
        P("fsdp", None, None),
        P("fsdp", None, None),
        P("fsdp", None, None),
        P(),
        P(),
    )
    out_specs = (P("fsdp", None, None), P("fsdp", None, None), P("fsdp", None, None))
    return jax.shard_map(body, mesh=mesh, in_specs=in_specs, out_specs=out_specs, check_vma=False)
```

time: 74.8 us -> 57.7 us (0.77)
  the two profiles are of different devices: /device:TPU:1 before, /device:TPU:129 now
where the time goes in v2:
time: 57.7 us; the launch traced here: 57.6 us
  Pallas kernels  56.9 us (99%)
  between operations  0.68 us (1%)
    pallas_call x1, Pallas kernels, body(): pl.pallas_call(functools.partial(gather_kernel, devices), out_shape=pltpu...  23.7 us
    pallas_call x1, Pallas kernels, body(): pl.pallas_call(functools.partial(return_kernel, devices), out_shape=[pltp...  21.4 us
    pallas_call x1, Pallas kernels, body(): pl.pallas_call(functools.partial(step_kernel, devices), grid_spec=pltpu.P...  10.1 us
    pallas_call x1, Pallas kernels, body(): pl.pallas_call(decode_kernel, grid=(slots,), out_shape=jax.ShapeDtypeStru...  1.73 us

profile of v2, /device:TPU:129, one launch (start us, length us, event | category | flops | bytes accessed | tf_op | source)
XLA Modules:
  0.0 57.6 jit_solution(4546560126193504118)
XLA Ops:
  0.6 0.0 copy-start
  0.6 0.0 copy-start.1
  0.7 23.7 %gather.1.gathered = bf16[5,4,256,256]{3,2,1,0:T(8,128)(2,1)S(1)} custom-call(bf16[1,4,256,256]{3,2,1,0:T(8,128)(2,1)} %grad.1), custom_call_target="tpu_custom_call" | custom-call | tf_op jit(solution)/shard_map/gather/pallas_call | solution.py:372
  24.3 0.0 copy-done
  24.4 0.0 copy-done.1
  24.4 10.1 %step.1 = (f32[6,256,256]{2,1,0:T(8,128)}, f32[6,256,256]{2,1,0:T(8,128)}, s16[5,4,128,256]{3,2,1,0:T(8,128)(2,1)S(1)}, f32[5,4,256]{2,1,0:T(4,128)S(1)}) custom-call(s32[128]{0:T(128)S(1)} %copy-done.1, s32[384]{0:T(512)S(1)} %copy-done, bf16[5,4,256,256]{3,2,1,0:T(8,128)(2,1)S(1)} %gather.1.gathered, f32[6,256,256]{2,1,0:T(8,128)} %moment.1, ...), custom_call_target="tpu_custom_call" | custom-call | tf_op jit(solution)/shard_map/step/pallas_call | solution.py:385
  34.4 21.4 %bring.1 = (s16[3,4,256,256]{3,2,1,0:T(8,128)(2,1)S(1)}, f32[3,2,4,256]{3,2,1,0:T(4,128)S(1)}) custom-call(s16[5,4,128,256]{3,2,1,0:T(8,128)(2,1)S(1)} %get-tuple-element.9.codes, f32[5,4,256]{2,1,0:T(4,128)S(1)} %get-tuple-element.10.scales), custom_call_target="tpu_custom_call" | custom-call | tf_op jit(solution)/shard_map/bring/pallas_call | solution.py:404
  55.9 1.7 %decode.1 = f32[4,256,256]{2,1,0:T(8,128)} custom-call(s16[3,4,256,256]{3,2,1,0:T(8,128)(2,1)S(1)} %get-tuple-element.11.codes, f32[3,2,4,256]{3,2,1,0:T(4,128)S(1)} %get-tuple-element.12.scales), custom_call_target="tpu_custom_call" | custom-call | tf_op jit(solution)/shard_map/decode/pallas_call | solution.py:424
Async XLA Ops:
  0.6 23.7 %copy-start = (s32[384]{0:T(512)S(1)}, s32[384]{0:T(512)}, u32[]{:S(2)}) copy-start(s32[384]{0:T(512)} %owners.1) | copy-start | bytes 4612
  0.6 23.7 %copy-start.1 = (s32[128]{0:T(128)S(1)}, s32[128]{0:T(128)}, u32[]{:S(2)}) copy-start(s32[128]{0:T(128)} %starts.1) | copy-start | bytes 1540

commit v3 on v2

v3 whole, which is shorter than its diff:
```python
import functools

import jax
import jax.numpy as jnp
from jax import lax
from jax.experimental import pallas as pl
from jax.experimental.pallas import tpu as pltpu
from jax.sharding import PartitionSpec as P

STEP = 10
BETA_ONE = 0.9
BETA_TWO = 0.95
EPSILON = 1e-08
TOP = 32766.0
ROOM = 40 * 2**20
MESH = pl.DeviceIdType.MESH
F32 = jnp.float32
BF16 = jnp.bfloat16
I16 = jnp.int16


def neighbours(devices):
    me = lax.axis_index("fsdp")
    core = lax.axis_index("dp")
    right = {"fsdp": jnp.minimum(me + 1, devices - 1)}
    left = {"fsdp": jnp.maximum(me - 1, 0)}
    twin = {"dp": 1 - core}
    return me, core, right, left, twin


def greet(me, devices, right, left, twin):
    barrier = pltpu.get_barrier_semaphore()

    def signal(peer):
        pl.semaphore_signal(barrier, inc=1, device_id=peer, device_id_type=MESH)

    signal(twin)
    pl.when(me < devices - 1)(lambda: signal(right))
    pl.when(me > 0)(lambda: signal(left))
    at_end = (me == 0) | (me == devices - 1)
    pl.when(at_end)(lambda: pl.semaphore_wait(barrier, 2))
    pl.when(~at_end)(lambda: pl.semaphore_wait(barrier, 3))


def push(src, dst, send_sem, recv_sem, peer):
    return pltpu.make_async_remote_copy(
        src_ref=src,
        dst_ref=dst,
        send_sem=send_sem,
        recv_sem=recv_sem,
        device_id=peer,
        device_id_type=MESH,
    )


def split(x):
    high = x.astype(BF16)
    return high, (x - high.astype(F32)).astype(BF16)


def dot(a, b, dims):
    return lax.dot_general(a, b, (dims, ((), ())), preferred_element_type=F32)


def dot_three(a, b, dims):
    return dot(a[0], b[0], dims) + (dot(a[0], b[1], dims) + dot(a[1], b[0], dims))


NN = ((1,), (0,))
NT = ((1,), (1,))
GROUP = 2


def soap_kernel(
    devices, starts_in, owners_in, grad, moment_in, second_in, left_in, right_in, first_out, second_out, out, out_scales,
    starts, owners, table, mine, theirs, other, gathered, moment, second, left, right, lt_high, lt_low, lh_high, lh_low, r_high, r_low, base,
    update, update_scales, codes, scales, far_in, far_scales, merged, merged_scales,
    load_sem, twin_sem, ring_send, ring_recv, hand_send, hand_recv, back_send, back_recv, near_send, near_recv, give_send, give_recv,
    sf_send, sf_recv, sr_send, sr_recv, sh_send, sh_recv
):
    me, core, right_peer, left_peer, twin = neighbours(devices)
    slots = grad.shape[1]
    half = grad.shape[2] // 2
    owned = moment.shape[0]
    blocks = owners.shape[0]
    rows = pl.ds(pl.multiple_of(core * half, half), half)
    other_rows = pl.ds(pl.multiple_of((1 - core) * half, half), half)

    loads = [
        pltpu.make_async_copy(src, dst, load_sem.at[at])
        for at, (src, dst) in enumerate(
            (
                (grad.at[0, :, other_rows], other),
                (grad.at[0, :, rows], mine),
                (starts_in, starts),
                (owners_in, owners),
                (left_in, left),
                (moment_in, moment),
                (right_in, right),
                (second_in, second),
            )
        )
    ]
    for load in loads:
        load.start()
    greet(me, devices, right_peer, left_peer, twin)

    loads[0].wait()
    swap = push(other, theirs, twin_sem.at[0], twin_sem.at[1], twin)
    swap.start()
    loads[1].wait()
    swap.wait_recv()
    for s in range(slots):
        gathered[2, s, rows] = (mine[s].astype(F32) + theirs[s].astype(F32)).astype(BF16)

    def part(k, s):
        return gathered.at[k, s, rows]

    def ring(src_k, dst_k, s, peer):
        return push(part(src_k, s), part(dst_k, s), ring_send.at[dst_k, s], ring_recv.at[dst_k, s], peer)

    def hand(k, s):
        return push(part(k, s), part(k, s), hand_send.at[k, s], hand_recv.at[k, s], twin)

    sides = (
        dict(at=0, near=1, far=0, peer=right_peer, has=me >= 1, gives=me >= 2, sends=me < devices - 1, to_far=4, to_near=3),
        dict(at=1, near=3, far=4, peer=left_peer, has=me < devices - 1, gives=me < devices - 2, sends=me >= 1, to_far=0, to_near=1),
    )
    for side in sides:

        @pl.when(side["sends"])
        def _():
            for s in range(slots):
                ring(2, side["near"], s, side["peer"]).start()

        @pl.when(~side["has"])
        def _():
            gathered[side["near"]] = jnp.zeros(gathered.shape[1:], BF16)
            far_in[side["at"]] = jnp.zeros(far_in.shape[1:], I16)
            far_scales[side["at"]] = jnp.zeros(far_scales.shape[1:], F32)
            out[side["at"]] = jnp.zeros(out.shape[1:], I16)
            out_scales[side["at"]] = jnp.zeros(out_scales.shape[1:], F32)

        @pl.when(~side["gives"])
        def _():
            gathered[side["far"]] = jnp.zeros(gathered.shape[1:], BF16)

    for s in range(slots):
        hand(2, s).start()

    loads[2].wait()
    loads[3].wait()

    def start_of(device):
        value = starts[jnp.clip(device, 0, devices - 1)]
        return jnp.where(device < 0, -1, jnp.where(device >= devices, blocks, value))

    first = jnp.maximum(start_of(me - 2), 0)
    below = jnp.int32(0)
    for k in range(5 * slots):
        at = first + k
        owner = owners[jnp.minimum(at, blocks - 1)]
        below += jnp.where((at < blocks) & (owner < me), 1, 0)
    first = first + below
    for j in range(owned):
        block = first + j
        live = (block < blocks) & (owners[jnp.minimum(block, blocks - 1)] == me)
        place = jnp.int32(0)
        for delta in (-1, 0, 1, 2):
            place += jnp.where(start_of(me + delta) <= block, 1, 0)
        slot = block - starts[jnp.clip(me + place - 2, 0, devices - 1)]
        table[0, j] = jnp.where(live, 1, 0)
        table[1, j] = jnp.where(live, jnp.clip(place, 0, 4), 0)
        table[2, j] = jnp.where(live, jnp.clip(slot, 0, slots - 1), 0)
    for k in range(5):
        holder = me + k - 2
        begin, end = start_of(holder), start_of(holder + 1)
        for s in range(slots):
            block = begin + s
            valid = (holder >= 0) & (holder < devices) & (block < end) & (owners[jnp.clip(block, 0, blocks - 1)] == me)
            table[3 + 2 * k, s] = jnp.where(valid, 1, 0)
            table[4 + 2 * k, s] = jnp.where(valid, jnp.clip(block - first, 0, owned - 1), 0)

    loads[4].wait()
    loads[5].wait()
    loads[6].wait()

    def prepare(j):
        whole = left[j]
        l_two = split(whole.T)
        r_two = split(right[j])
        h_two = split(left[j, rows])
        lt_high[j], lt_low[j] = l_two
        r_high[j], r_low[j] = r_two
        lh_high[j], lh_low[j] = h_two
        turned = dot_three(split(dot_three(l_two, split(moment[j]), NN)), r_two, NN)
        base[j] = BETA_ONE * turned

    def relay(s):
        for side in sides:

            @pl.when(side["has"])
            def _():
                ring(2, side["near"], s, side["peer"]).wait_recv()

            @pl.when(side["has"] & side["sends"])
            def _():
                ring(side["near"], side["far"], s, side["peer"]).start()

            @pl.when(side["has"])
            def _():
                hand(side["near"], s).start()

    @pl.loop(0, owned)
    def _(j):
        prepare(j)

        @pl.when(j >= owned - slots)
        def _():
            relay(j - (owned - slots))

    loads[7].wait()
    for s in range(slots):
        for side in sides:

            @pl.when(side["gives"])
            def _():
                ring(side["near"], side["far"], s, side["peer"]).wait_recv()
                hand(side["far"], s).start()

    swap.wait_send()
    for s in range(slots):
        hand(2, s).wait_send()
        hand(2, s).wait_recv()
    for side in sides:

        @pl.when(side["sends"])
        def _():
            for s in range(slots):
                ring(2, side["near"], s, side["peer"]).wait_send()

        @pl.when(side["has"] & side["sends"])
        def _():
            for s in range(slots):
                ring(side["near"], side["far"], s, side["peer"]).wait_send()

        @pl.when(side["has"])
        def _():
            for s in range(slots):
                hand(side["near"], s).wait_send()
                hand(side["near"], s).wait_recv()

        @pl.when(side["gives"])
        def _():
            for s in range(slots):
                hand(side["far"], s).wait_send()
                hand(side["far"], s).wait_recv()

    def solve(j):
        live = table[0, j] == 1
        gradient = gathered[table[1, j], table[2, j]]
        r_two = (r_high[j], r_low[j])
        first_out[j] = jnp.where(live, BETA_ONE * moment[j] + (1.0 - BETA_ONE) * gradient.astype(F32), 0.0)
        half_turned = dot(lt_high[j], gradient, NN) + dot(lt_low[j], gradient, NN)
        turned = dot_three(split(half_turned), r_two, NN)
        second_next = BETA_TWO * second[j] + (1.0 - BETA_TWO) * turned * turned
        second_out[j] = jnp.where(live, second_next, 0.0)
        bias_one = 1.0 - BETA_ONE**STEP
        bias_two = 1.0 - BETA_TWO**STEP
        turned_moment = base[j] + (1.0 - BETA_ONE) * turned
        scaled = turned_moment * (1.0 / bias_one) / (jnp.sqrt(second_next * (1.0 / bias_two)) + EPSILON)
        new = dot_three(split(dot_three((lh_high[j], lh_low[j]), split(scaled), NN)), r_two, NT)
        largest = jnp.maximum(jnp.max(jnp.abs(new), axis=0, keepdims=True), 1e-30)
        update[j] = jnp.round(new * (TOP / largest)).astype(jnp.int32).astype(I16)
        update_scales[j] = largest * (1.0 / TOP)

    @pl.loop(0, owned // GROUP)
    def _(step):
        for at in range(GROUP):
            solve(step * GROUP + at)

    def chosen(k, s, absent):
        return jnp.where(table[3 + 2 * k, s] == 1, update[table[4 + 2 * k, s]], absent)

    def chosen_scale(k, s, absent):
        return jnp.where(table[3 + 2 * k, s] == 1, update_scales[table[4 + 2 * k, s]], absent)

    def far(side, s):
        at = side["at"]
        return push(codes.at[at, s], far_in.at[at, s], back_send.at[at, s], back_recv.at[at, s], side["peer"])

    def far_scale(side):
        at = side["at"]
        return push(scales.at[at], far_scales.at[at], sf_send.at[at], sf_recv.at[at], side["peer"])

    def near(side, s):
        at = side["at"]
        return push(merged.at[at, s], out.at[at, s, rows], near_send.at[at, s], near_recv.at[at, s], side["peer"])

    def near_scale(side):
        at = side["at"]
        return push(merged_scales.at[at], out_scales.at[at, core], sr_send.at[at], sr_recv.at[at], side["peer"])

    def give(k, s):
        return push(out.at[k, s, rows], out.at[k, s, rows], give_send.at[k, s], give_recv.at[k, s], twin)

    def give_scale(k):
        return push(out_scales.at[k, core], out_scales.at[k, core], sh_send.at[k], sh_recv.at[k], twin)

    for s in range(slots):
        for side in sides:
            codes[side["at"], s] = chosen(side["to_far"], s, jnp.zeros((), I16))
            pl.when(side["sends"])(far(side, s).start)
    for side in sides:
        for s in range(slots):
            scales[side["at"], pl.ds(s, 1)] = chosen_scale(side["to_far"], s, 0.0)
        pl.when(side["sends"])(far_scale(side).start)
    for s in range(slots):
        out[2, s, rows] = chosen(2, s, jnp.zeros((), I16))
        give(2, s).start()
        out_scales[2, core, pl.ds(s, 1)] = chosen_scale(2, s, 0.0)
    give_scale(2).start()
    for s in range(slots):
        for side in sides:
            pl.when(side["has"])(far(side, s).wait_recv)
            merged[side["at"], s] = chosen(side["to_near"], s, far_in[side["at"], s])
            pl.when(side["sends"])(near(side, s).start)
    for side in sides:
        pl.when(side["has"])(far_scale(side).wait_recv)
        for s in range(slots):
            merged_scales[side["at"], pl.ds(s, 1)] = chosen_scale(side["to_near"], s, far_scales[side["at"], pl.ds(s, 1)])
        pl.when(side["sends"])(near_scale(side).start)
    for s in range(slots):
        for side in sides:

            @pl.when(side["has"])
            def _():
                near(side, s).wait_recv()
                give(side["at"], s).start()

    for side in sides:

        @pl.when(side["has"])
        def _():
            near_scale(side).wait_recv()
            give_scale(side["at"]).start()

    give_scale(2).wait_send()
    give_scale(2).wait_recv()
    for s in range(slots):
        give(2, s).wait_send()
        give(2, s).wait_recv()
    for side in sides:

        @pl.when(side["sends"])
        def _():
            far_scale(side).wait_send()
            near_scale(side).wait_send()
            for s in range(slots):
                far(side, s).wait_send()
                near(side, s).wait_send()

        @pl.when(side["has"])
        def _():
            give_scale(side["at"]).wait_send()
            give_scale(side["at"]).wait_recv()
            for s in range(slots):
                give(side["at"], s).wait_send()
                give(side["at"], s).wait_recv()


def finish_kernel(codes, scales, first, second, direction, first_new, second_new, decoded, sem):
    slots = codes.shape[1]
    half = codes.shape[2] // 2
    copies = [pltpu.make_async_copy(first, first_new, sem.at[0]), pltpu.make_async_copy(second, second_new, sem.at[1])]
    for copy in copies:
        copy.start()
    for s in range(slots):
        for core in range(2):
            rows = pl.ds(core * half, half)
            total = 0.0
            for k in range(3):
                total += codes[k, s, rows].astype(jnp.int32).astype(F32) * scales[k, core, pl.ds(s, 1)]
            decoded[s, rows] = total
        copy = pltpu.make_async_copy(decoded.at[s], direction.at[s], sem.at[2 + s])
        copy.start()
        copies.append(copy)
    for copy in copies:
        copy.wait()


def body(gradients, first_moment, second_moment, left_basis, right_basis, shard_starts, block_owners):
    devices = lax.axis_size("fsdp")
    slots = gradients.shape[1]
    owned, width = first_moment.shape[0], first_moment.shape[1]
    half = width // 2
    any_space = pl.BlockSpec(memory_space=pl.ANY)
    in_vmem = pl.BlockSpec(memory_space=pltpu.VMEM)
    dma = pltpu.SemaphoreType.DMA
    keep = functools.partial(pltpu.with_memory_space_constraint, memory_space=pltpu.VMEM)
    stay = functools.partial(pltpu.with_memory_space_constraint, memory_space=pltpu.HBM)
    matrices = (owned, width, width)
    halves = (owned, half, width)
    first_new, second_new, out, out_scales = pl.pallas_call(
        functools.partial(soap_kernel, devices),
        out_shape=[
            pltpu.VMEM(matrices, F32),
            pltpu.VMEM(matrices, F32),
            pltpu.VMEM((3, slots, width, width), I16),
            pltpu.VMEM((3, 2, slots, width), F32),
        ],
        in_specs=[any_space] * 7,
        out_specs=[in_vmem] * 4,
        scratch_shapes=[
            pltpu.SMEM(shard_starts.shape, jnp.int32),
            pltpu.SMEM(block_owners.shape, jnp.int32),
            pltpu.SMEM((13, 8), jnp.int32),
            *[pltpu.VMEM((slots, half, width), BF16)] * 3,
            pltpu.VMEM((5, slots, width, width), BF16),
            *[pltpu.VMEM(matrices, F32)] * 4,
            *[pltpu.VMEM(matrices, BF16)] * 2,
            *[pltpu.VMEM(halves, BF16)] * 2,
            *[pltpu.VMEM(matrices, BF16)] * 2,
            pltpu.VMEM(matrices, F32),
            pltpu.VMEM(halves, I16),
            pltpu.VMEM((owned, 1, width), F32),
            *[pltpu.VMEM((2, slots, half, width), I16), pltpu.VMEM((2, slots, width), F32)] * 3,
            dma((8,)), dma((2,)), *[dma((5, slots))] * 4, *[dma((2, slots))] * 4, *[dma((3, slots))] * 2, *[dma((2,))] * 4, *[dma((3,))] * 2,
        ],
        compiler_params=pltpu.CompilerParams(collective_id=0, has_side_effects=True, vmem_limit_bytes=ROOM),
        name="soap",
    )(*map(stay, (shard_starts, block_owners, gradients, first_moment, second_moment, left_basis, right_basis)))

    return tuple(
        pl.pallas_call(
            finish_kernel,
            out_shape=[
                jax.ShapeDtypeStruct((slots, width, width), F32),
                jax.ShapeDtypeStruct(matrices, F32),
                jax.ShapeDtypeStruct(matrices, F32),
            ],
            in_specs=[in_vmem] * 4,
            out_specs=[any_space] * 3,
            scratch_shapes=[pltpu.VMEM((slots, width, width), F32), dma((2 + slots,))],
            compiler_params=pltpu.CompilerParams(vmem_limit_bytes=8 * 2**20),
            name="finish",
        )(*map(keep, (out, out_scales, first_new, second_new)))
    )


def solution(mesh):
    in_specs = (
        P("dp", "fsdp", None, None),
        P("fsdp", None, None),
        P("fsdp", None, None),
        P("fsdp", None, None),
        P("fsdp", None, None),
        P(),
        P(),
    )
    out_specs = (P("fsdp", None, None), P("fsdp", None, None), P("fsdp", None, None))
    return jax.shard_map(body, mesh=mesh, in_specs=in_specs, out_specs=out_specs, check_vma=False)
```

time: 57.7 us -> 50.6 us (0.88)
  Pallas kernels: 56.9 us -> 49.9 us
    pallas_call x4 -> x2, Pallas kernels: 56.9 us -> 49.9 us  [the longest x1 47.8 us: body(): pl.pallas_call(functools.partial(soap_kernel, devices), out_shape=[pltpu....]
where the time goes in v3:
time: 50.6 us; the launch traced here: 50.5 us
  Pallas kernels  49.9 us (99%)
  between operations  0.64 us (1%)
    pallas_call x1, Pallas kernels, body(): pl.pallas_call(functools.partial(soap_kernel, devices), out_shape=[pltpu....  47.8 us
    pallas_call x1, Pallas kernels, body(): pl.pallas_call(finish_kernel, out_shape=[jax.ShapeDtypeStruct((slots, wid...  2.05 us

profile of v3, /device:TPU:129, one launch (start us, length us, event | category | flops | bytes accessed | tf_op | source)
XLA Modules:
  0.0 50.5 jit_solution(6625806281480548352)
XLA Ops:
  0.6 47.8 %soap.1 = (f32[6,256,256]{2,1,0:T(8,128)S(1)}, f32[6,256,256]{2,1,0:T(8,128)S(1)}, s16[3,4,256,256]{3,2,1,0:T(8,128)(2,1)S(1)}, f32[3,2,4,256]{3,2,1,0:T(4,128)S(1)}) custom-call(s32[128]{0:T(128)} %starts_in.1, s32[384]{0:T(512)} %owners_in.1, bf16[1,4,256,256]{3,2,1,0:T(8,128)(2,1)} %grad.1, f32[6,256,256]{2,1,0:T(8,128)} %moment_in.1, ...), custom_call_target="tpu_custom_call" | custom-call | tf_op jit(solution)/shard_map/soap/pallas_call | solution.py:404
  48.5 2.1 %finish.1 = (f32[4,256,256]{2,1,0:T(8,128)}, f32[6,256,256]{2,1,0:T(8,128)}, f32[6,256,256]{2,1,0:T(8,128)}) custom-call(s16[3,4,256,256]{3,2,1,0:T(8,128)(2,1)S(1)} %get-tuple-element.7.codes, f32[3,2,4,256]{3,2,1,0:T(4,128)S(1)} %get-tuple-element.8.scales, f32[6,256,256]{2,1,0:T(8,128)S(1)} %get-tuple-element.9.first, ...), custom_call_target="tpu_custom_call" | custom-call | tf_op jit(solution)/shard_map/finish/pallas_call | solution.py:435

commit v4 on v3

v4 whole, which is shorter than its diff:
```python
import functools

import jax
import jax.numpy as jnp
from jax import lax
from jax.experimental import pallas as pl
from jax.experimental.pallas import tpu as pltpu
from jax.sharding import PartitionSpec as P

STEP = 10
BETA_ONE = 0.9
BETA_TWO = 0.95
EPSILON = 1e-08
TOP = 32766.0
ROOM = 40 * 2**20
MESH = pl.DeviceIdType.MESH
F32 = jnp.float32
BF16 = jnp.bfloat16
I16 = jnp.int16


def neighbours(devices):
    me = lax.axis_index("fsdp")
    core = lax.axis_index("dp")
    right = {"fsdp": jnp.minimum(me + 1, devices - 1)}
    left = {"fsdp": jnp.maximum(me - 1, 0)}
    twin = {"dp": 1 - core}
    return me, core, right, left, twin


def greet(me, devices, right, left, twin):
    barrier = pltpu.get_barrier_semaphore()

    def signal(peer):
        pl.semaphore_signal(barrier, inc=1, device_id=peer, device_id_type=MESH)

    signal(twin)
    pl.when(me < devices - 1)(lambda: signal(right))
    pl.when(me > 0)(lambda: signal(left))
    at_end = (me == 0) | (me == devices - 1)
    pl.when(at_end)(lambda: pl.semaphore_wait(barrier, 2))
    pl.when(~at_end)(lambda: pl.semaphore_wait(barrier, 3))


def push(src, dst, send_sem, recv_sem, peer):
    return pltpu.make_async_remote_copy(
        src_ref=src,
        dst_ref=dst,
        send_sem=send_sem,
        recv_sem=recv_sem,
        device_id=peer,
        device_id_type=MESH,
    )


def split(x):
    high = x.astype(BF16)
    return high, (x - high.astype(F32)).astype(BF16)


def dot(a, b, dims):
    return lax.dot_general(a, b, (dims, ((), ())), preferred_element_type=F32)


def dot_three(a, b, dims):
    return dot(a[0], b[0], dims) + (dot(a[0], b[1], dims) + dot(a[1], b[0], dims))


NN = ((1,), (0,))
NT = ((1,), (1,))
GROUP = 2
WAVE = 2
LATE = 4


def soap_kernel(
    devices, starts_in, owners_in, grad, moment_in, second_in, left_in, right_in, first_out, second_out, out, out_scales,
    starts, owners, table, mine, theirs, other, gathered_a, gathered_b, moment, second, left, right, lt_high, lt_low, lh_high, lh_low, r_high, r_low,
    base, update_a, update_b, scales_a, scales_b, second_late, codes, scales, far_in, far_scales, merged, merged_scales,
    load_sem, swap_send, swap_recv, own_send, relay_send, ring_recv, hand_send, hand_recv, far_send, far_recv, near_send, near_recv, give_send, give_recv,
    sf_send, sf_recv, sr_send, sr_recv, sh_send, sh_recv
):
    me, core, right_peer, left_peer, twin = neighbours(devices)
    slots = grad.shape[1]
    half = grad.shape[2] // 2
    owned = moment.shape[0]
    blocks = owners.shape[0]
    rows = pl.ds(pl.multiple_of(core * half, half), half)
    other_rows = pl.ds(pl.multiple_of((1 - core) * half, half), half)
    gathered = (gathered_a, gathered_b)

    loads = [
        pltpu.make_async_copy(src, dst, load_sem.at[at])
        for at, (src, dst) in enumerate(
            (
                (grad.at[0, :, other_rows], other),
                (grad.at[0, :, rows], mine),
                (starts_in, starts),
                (owners_in, owners),
                (left_in, left),
                (moment_in, moment),
                (right_in, right),
                (second_in, second),
            )
        )
    ]
    for load in loads:
        load.start()
    greet(me, devices, right_peer, left_peer, twin)

    def swap(w):
        part = pl.ds(WAVE * w, WAVE)
        return push(other.at[part], theirs.at[part], swap_send.at[w], swap_recv.at[w], twin)

    def own(w, side, t):
        source = gathered[w].at[2, t, rows] if t is not None else gathered[w].at[2, :, rows]
        target = gathered[w].at[side["near"], t, rows] if t is not None else gathered[w].at[side["near"], :, rows]
        arrived = ring_recv.at[side["near"], WAVE * w + (t or 0)]
        return push(source, target, own_send.at[side["at"], w], arrived, side["peer"])

    def relay(w, side, t):
        source = gathered[w].at[side["near"], t, rows] if t is not None else gathered[w].at[side["near"], :, rows]
        target = gathered[w].at[side["far"], t, rows] if t is not None else gathered[w].at[side["far"], :, rows]
        arrived = ring_recv.at[side["far"], WAVE * w + (t or 0)]
        return push(source, target, relay_send.at[side["at"], w], arrived, side["peer"])

    def hand(w, k, t):
        part = gathered[w].at[k, t, rows] if t is not None else gathered[w].at[k, :, rows]
        return push(part, part, hand_send.at[w, k], hand_recv.at[w, k], twin)

    to_right = dict(at=0, near=1, far=0, peer=right_peer, has=me >= 1, gives=me >= 2, sends=me < devices - 1, to_far=4, to_near=3)
    to_left = dict(at=1, near=3, far=4, peer=left_peer, has=me < devices - 1, gives=me < devices - 2, sends=me >= 1, to_far=0, to_near=1)
    sides = (to_right, to_left)

    def send_own(w, side):
        @pl.when(side["sends"])
        def _():
            for t in range(WAVE):
                own(w, side, t).start()

    def send_on(w, side):
        for t in range(WAVE):

            @pl.when(side["has"])
            def _():
                own(w, side, t).wait_recv()

            @pl.when(side["has"] & side["sends"])
            def _():
                relay(w, side, t).start()

            @pl.when(side["has"])
            def _():
                hand(w, side["near"], t).start()

    def add_up(w):
        swap(w).wait_recv()
        for t in range(WAVE):
            s = WAVE * w + t
            gathered[w][2, t, rows] = (mine[s].astype(F32) + theirs[s].astype(F32)).astype(BF16)

    loads[0].wait()
    swap(0).start()
    swap(1).start()
    loads[1].wait()
    add_up(0)
    for side in sides:
        send_own(0, side)
    for t in range(WAVE):
        hand(0, 2, t).start()
    add_up(1)
    for t in range(WAVE):
        hand(1, 2, t).start()

    for side in sides:

        @pl.when(~side["has"])
        def _():
            far_in[side["at"]] = jnp.zeros(far_in.shape[1:], I16)
            far_scales[side["at"]] = jnp.zeros(far_scales.shape[1:], F32)
            out[side["at"]] = jnp.zeros(out.shape[1:], I16)
            out_scales[side["at"]] = jnp.zeros(out_scales.shape[1:], F32)
            for w in range(2):
                gathered[w][side["near"]] = jnp.zeros(gathered[w].shape[1:], BF16)

        @pl.when(~side["gives"])
        def _():
            for w in range(2):
                gathered[w][side["far"]] = jnp.zeros(gathered[w].shape[1:], BF16)

    loads[2].wait()
    loads[3].wait()

    def start_of(device):
        value = starts[jnp.clip(device, 0, devices - 1)]
        return jnp.where(device < 0, -1, jnp.where(device >= devices, blocks, value))

    first = jnp.maximum(start_of(me - 2), 0)
    below = jnp.int32(0)
    for k in range(5 * slots):
        at = first + k
        owner = owners[jnp.minimum(at, blocks - 1)]
        below += jnp.where((at < blocks) & (owner < me), 1, 0)
    first = first + below
    rank = jnp.int32(0)
    chosen_late = [jnp.int32(0)] * LATE
    for j in range(owned):
        block = first + j
        live = (block < blocks) & (owners[jnp.minimum(block, blocks - 1)] == me)
        place = jnp.int32(0)
        for delta in (-1, 0, 1, 2):
            place += jnp.where(start_of(me + delta) <= block, 1, 0)
        slot = block - starts[jnp.clip(me + place - 2, 0, devices - 1)]
        late = live & (slot >= WAVE)
        table[0, j] = jnp.where(live & ~late, 1, 0)
        table[1, j] = jnp.where(late, 1, 0)
        table[2, j] = jnp.where(live, jnp.clip(place, 0, 4), 0)
        table[3, j] = jnp.where(live, jnp.clip(lax.rem(slot, WAVE), 0, WAVE - 1), 0)
        table[4, j] = rank
        for b in range(LATE):
            chosen_late[b] = jnp.where(late & (rank == b), j, chosen_late[b])
        rank = jnp.minimum(rank + jnp.where(late, 1, 0), LATE - 1)
    for b in range(LATE):
        table[5, b] = chosen_late[b]
    for k in range(5):
        holder = me + k - 2
        begin, end = start_of(holder), start_of(holder + 1)
        for s in range(slots):
            block = begin + s
            valid = (holder >= 0) & (holder < devices) & (block < end) & (owners[jnp.clip(block, 0, blocks - 1)] == me)
            table[6 + 2 * k, s] = jnp.where(valid, 1, 0)
            table[7 + 2 * k, s] = jnp.where(valid, jnp.clip(block - first, 0, owned - 1), 0)

    loads[4].wait()
    loads[5].wait()
    loads[6].wait()

    def prepare(j):
        whole = left[j]
        l_two = split(whole.T)
        r_two = split(right[j])
        h_two = split(left[j, rows])
        lt_high[j], lt_low[j] = l_two
        r_high[j], r_low[j] = r_two
        lh_high[j], lh_low[j] = h_two
        turned = dot_three(split(dot_three(l_two, split(moment[j]), NN)), r_two, NN)
        base[j] = BETA_ONE * turned

    place_in_plane = lax.rem(me, 16)
    z_left, z_right = place_in_plane == 0, place_in_plane == 15
    z_edge = z_left | z_right
    x_left = (lax.rem(me, 4) == 0) & ~z_left

    def middle(first_side, second_side):
        for side in (first_side, second_side):
            send_on(0, side)
            send_own(1, side)

    def middle_at_edge(early, late):
        send_own(1, late)
        send_on(0, early)
        send_own(1, early)
        send_on(1, early)
        send_on(0, late)

    @pl.loop(0, owned // 2)
    def _(j):
        prepare(j)

    pl.when(z_left)(lambda: middle_at_edge(to_left, to_right))
    pl.when(z_right)(lambda: middle_at_edge(to_right, to_left))
    pl.when(x_left)(lambda: middle(to_left, to_right))
    pl.when(~z_edge & ~x_left)(lambda: middle(to_right, to_left))

    @pl.loop(owned // 2, owned)
    def _(j):
        prepare(j)

    loads[7].wait()

    def arrive(w):
        for t in range(WAVE):
            for side in sides:

                @pl.when(side["gives"])
                def _():
                    relay(w, side, t).wait_recv()
                    hand(w, side["far"], t).start()

        hand(w, 2, None).wait_recv()
        for side in sides:

            @pl.when(side["has"])
            def _():
                hand(w, side["near"], None).wait_recv()

            @pl.when(side["gives"])
            def _():
                hand(w, side["far"], None).wait_recv()

    def solve(j, gradient):
        r_two = (r_high[j], r_low[j])
        half_turned = dot(lt_high[j], gradient, NN) + dot(lt_low[j], gradient, NN)
        turned = dot_three(split(half_turned), r_two, NN)
        second_next = BETA_TWO * second[j] + (1.0 - BETA_TWO) * turned * turned
        bias_one = 1.0 - BETA_ONE**STEP
        bias_two = 1.0 - BETA_TWO**STEP
        turned_moment = base[j] + (1.0 - BETA_ONE) * turned
        scaled = turned_moment * (1.0 / bias_one) / (jnp.sqrt(second_next * (1.0 / bias_two)) + EPSILON)
        new = dot_three(split(dot_three((lh_high[j], lh_low[j]), split(scaled), NN)), r_two, NT)
        largest = jnp.maximum(jnp.max(jnp.abs(new), axis=0, keepdims=True), 1e-30)
        return second_next, jnp.round(new * (TOP / largest)).astype(jnp.int32).astype(I16), largest * (1.0 / TOP)

    arrive(0)

    @pl.loop(0, owned // GROUP)
    def _(step):
        @pl.when((step == 1) & ~z_left)
        def _():
            pl.when(~z_right)(lambda: send_on(1, to_right))
            send_on(1, to_left)

        @pl.when((step == 1) & z_left)
        def _():
            send_on(1, to_right)

        for at in range(GROUP):
            j = step * GROUP + at
            second_out[j], update_a[j], scales_a[j] = solve(j, gathered_a[table[2, j], table[3, j]])

    def chosen(k, s, absent):
        at = table[7 + 2 * k, s]
        value = update_a[at] if s < WAVE else update_b[table[4, at]]
        return jnp.where(table[6 + 2 * k, s] == 1, value, absent)

    def chosen_scale(k, s, absent):
        at = table[7 + 2 * k, s]
        value = scales_a[at] if s < WAVE else scales_b[table[4, at]]
        return jnp.where(table[6 + 2 * k, s] == 1, value, absent)

    def far(w, side, t):
        at = side["at"]
        part = (at, w, t) if t is not None else (at, w)
        return push(codes.at[part], far_in.at[part], far_send.at[at, w], far_recv.at[at, WAVE * w + (t or 0)], side["peer"])

    def far_scale(w, side):
        at = side["at"]
        return push(scales.at[at, w], far_scales.at[at, w], sf_send.at[at, w], sf_recv.at[at, w], side["peer"])

    def near(w, side, t):
        at = side["at"]
        part = (at, w, t) if t is not None else (at, w)
        held = (at, WAVE * w + t, rows) if t is not None else (at, pl.ds(WAVE * w, WAVE), rows)
        return push(merged.at[part], out.at[held], near_send.at[at, w], near_recv.at[at, WAVE * w + (t or 0)], side["peer"])

    def near_scale(w, side):
        at = side["at"]
        return push(merged_scales.at[at, w], out_scales.at[at, core, w], sr_send.at[at, w], sr_recv.at[at, w], side["peer"])

    def give(k, s):
        part = out.at[k, s, rows] if s is not None else out.at[k, :, rows]
        return push(part, part, give_send.at[k], give_recv.at[k], twin)

    def give_scale(k):
        return push(out_scales.at[k, core], out_scales.at[k, core], sh_send.at[k], sh_recv.at[k], twin)

    def send_far(w):
        for t in range(WAVE):
            for side in sides:
                codes[side["at"], w, t] = chosen(side["to_far"], WAVE * w + t, jnp.zeros((), I16))
                pl.when(side["sends"])(far(w, side, t).start)
        for side in sides:
            for t in range(WAVE):
                scales[side["at"], w, pl.ds(t, 1)] = chosen_scale(side["to_far"], WAVE * w + t, 0.0)
            pl.when(side["sends"])(far_scale(w, side).start)
        for t in range(WAVE):
            s = WAVE * w + t
            out[2, s, rows] = chosen(2, s, jnp.zeros((), I16))
            give(2, s).start()
            out_scales[2, core, w, pl.ds(t, 1)] = chosen_scale(2, s, 0.0)

    def send_near(w, side):
        for t in range(WAVE):
            pl.when(side["has"])(far(w, side, t).wait_recv)
            merged[side["at"], w, t] = chosen(side["to_near"], WAVE * w + t, far_in[side["at"], w, t])
            pl.when(side["sends"])(near(w, side, t).start)
        pl.when(side["has"])(far_scale(w, side).wait_recv)
        for t in range(WAVE):
            merged_scales[side["at"], w, pl.ds(t, 1)] = chosen_scale(
                side["to_near"], WAVE * w + t, far_scales[side["at"], w, pl.ds(t, 1)]
            )
        pl.when(side["sends"])(near_scale(w, side).start)

    send_far(0)
    arrive(1)

    @pl.loop(0, LATE // GROUP)
    def _(step):
        for at in range(GROUP):
            b = step * GROUP + at
            j = table[5, b]
            second_late[b], update_b[b], scales_b[b] = solve(j, gathered_b[table[2, j], table[3, j]])

    send_far(1)
    give_scale(2).start()

    def send_all_near(order):
        for w, side in order:
            send_near(w, side)

    pl.when(z_left)(lambda: send_all_near(((0, to_left), (1, to_left), (0, to_right), (1, to_right))))
    pl.when(z_right)(lambda: send_all_near(((0, to_right), (1, to_right), (0, to_left), (1, to_left))))
    pl.when(x_left)(lambda: send_all_near(((0, to_left), (0, to_right), (1, to_left), (1, to_right))))
    pl.when(~z_edge & ~x_left)(lambda: send_all_near(((0, to_right), (0, to_left), (1, to_right), (1, to_left))))

    @pl.loop(0, owned)
    def _(j):
        early, late = table[0, j] == 1, table[1, j] == 1
        gradient = jnp.where(late, gathered_b[table[2, j], table[3, j]].astype(F32), gathered_a[table[2, j], table[3, j]].astype(F32))
        first_out[j] = jnp.where(early | late, BETA_ONE * moment[j] + (1.0 - BETA_ONE) * gradient, 0.0)
        second_out[j] = jnp.where(late, second_late[table[4, j]], jnp.where(early, second_out[j], 0.0))

    for s in range(slots):
        for side in sides:

            @pl.when(side["has"])
            def _():
                near(s // WAVE, side, s % WAVE).wait_recv()
                give(side["at"], s).start()

    for side in sides:

        @pl.when(side["has"])
        def _():
            for w in range(2):
                near_scale(w, side).wait_recv()
            give_scale(side["at"]).start()

    for w in range(2):
        swap(w).wait_send()
        hand(w, 2, None).wait_send()
    give(2, None).wait_send()
    give_scale(2).wait_send()
    for side in sides:

        @pl.when(side["sends"])
        def _():
            for w in range(2):
                own(w, side, None).wait_send()
                far(w, side, None).wait_send()
                far_scale(w, side).wait_send()
                near(w, side, None).wait_send()
                near_scale(w, side).wait_send()

        @pl.when(side["has"] & side["sends"])
        def _():
            for w in range(2):
                relay(w, side, None).wait_send()

        @pl.when(side["has"])
        def _():
            for w in range(2):
                hand(w, side["near"], None).wait_send()
            give(side["at"], None).wait_send()
            give_scale(side["at"]).wait_send()

        @pl.when(side["gives"])
        def _():
            for w in range(2):
                hand(w, side["far"], None).wait_send()

    give(2, None).wait_recv()
    give_scale(2).wait_recv()
    for side in sides:

        @pl.when(side["has"])
        def _():
            give(side["at"], None).wait_recv()
            give_scale(side["at"]).wait_recv()


def finish_kernel(codes, scales, first, second, direction, first_new, second_new, decoded, sem):
    slots = codes.shape[1]
    half = codes.shape[2] // 2
    copies = [pltpu.make_async_copy(first, first_new, sem.at[0]), pltpu.make_async_copy(second, second_new, sem.at[1])]
    for copy in copies:
        copy.start()
    for s in range(slots):
        for core in range(2):
            rows = pl.ds(core * half, half)
            total = 0.0
            for k in range(3):
                total += codes[k, s, rows].astype(jnp.int32).astype(F32) * scales[k, core, s // WAVE, pl.ds(s % WAVE, 1)]
            decoded[s, rows] = total
        copy = pltpu.make_async_copy(decoded.at[s], direction.at[s], sem.at[2 + s])
        copy.start()
        copies.append(copy)
    for copy in copies:
        copy.wait()


def body(gradients, first_moment, second_moment, left_basis, right_basis, shard_starts, block_owners):
    devices = lax.axis_size("fsdp")
    slots = gradients.shape[1]
    owned, width = first_moment.shape[0], first_moment.shape[1]
    half = width // 2
    any_space = pl.BlockSpec(memory_space=pl.ANY)
    in_vmem = pl.BlockSpec(memory_space=pltpu.VMEM)
    dma = pltpu.SemaphoreType.DMA
    keep = functools.partial(pltpu.with_memory_space_constraint, memory_space=pltpu.VMEM)
    stay = functools.partial(pltpu.with_memory_space_constraint, memory_space=pltpu.HBM)
    matrices = (owned, width, width)
    halves = (owned, half, width)
    first_new, second_new, out, out_scales = pl.pallas_call(
        functools.partial(soap_kernel, devices),
        out_shape=[
            pltpu.VMEM(matrices, F32),
            pltpu.VMEM(matrices, F32),
            pltpu.VMEM((3, slots, width, width), I16),
            pltpu.VMEM((3, 2, 2, WAVE, width), F32),
        ],
        in_specs=[any_space] * 7,
        out_specs=[in_vmem] * 4,
        scratch_shapes=[
            pltpu.SMEM(shard_starts.shape, jnp.int32),
            pltpu.SMEM(block_owners.shape, jnp.int32),
            pltpu.SMEM((16, 8), jnp.int32),
            *[pltpu.VMEM((slots, half, width), BF16)] * 3,
            *[pltpu.VMEM((5, WAVE, width, width), BF16)] * 2,
            *[pltpu.VMEM(matrices, F32)] * 4,
            *[pltpu.VMEM(matrices, BF16)] * 2,
            *[pltpu.VMEM(halves, BF16)] * 2,
            *[pltpu.VMEM(matrices, BF16)] * 2,
            pltpu.VMEM(matrices, F32),
            pltpu.VMEM(halves, I16),
            pltpu.VMEM((LATE, half, width), I16),
            pltpu.VMEM((owned, 1, width), F32),
            pltpu.VMEM((LATE, 1, width), F32),
            pltpu.VMEM((LATE, width, width), F32),
            *[pltpu.VMEM((2, 2, WAVE, half, width), I16), pltpu.VMEM((2, 2, WAVE, width), F32)] * 3,
            dma((8,)), *[dma((2,))] * 2, *[dma((2, 2))] * 2, dma((5, slots)), *[dma((2, 5))] * 2,
            *[dma((2, 2)), dma((2, slots))] * 2, *[dma((3,))] * 2, *[dma((2, 2))] * 4, *[dma((3,))] * 2,
        ],
        compiler_params=pltpu.CompilerParams(collective_id=0, has_side_effects=True, vmem_limit_bytes=ROOM),
        name="soap",
    )(*map(stay, (shard_starts, block_owners, gradients, first_moment, second_moment, left_basis, right_basis)))

    return tuple(
        pl.pallas_call(
            finish_kernel,
            out_shape=[
                jax.ShapeDtypeStruct((slots, width, width), F32),
                jax.ShapeDtypeStruct(matrices, F32),
                jax.ShapeDtypeStruct(matrices, F32),
            ],
            in_specs=[in_vmem] * 4,
            out_specs=[any_space] * 3,
            scratch_shapes=[pltpu.VMEM((slots, width, width), F32), dma((2 + slots,))],
            compiler_params=pltpu.CompilerParams(vmem_limit_bytes=8 * 2**20),
            name="finish",
        )(*map(keep, (out, out_scales, first_new, second_new)))
    )


def solution(mesh):
    in_specs = (
        P("dp", "fsdp", None, None),
        P("fsdp", None, None),
        P("fsdp", None, None),
        P("fsdp", None, None),
        P("fsdp", None, None),
        P(),
        P(),
    )
    out_specs = (P("fsdp", None, None), P("fsdp", None, None), P("fsdp", None, None))
    return jax.shard_map(body, mesh=mesh, in_specs=in_specs, out_specs=out_specs, check_vma=False)
```

time: 50.6 us -> 52.9 us (1.045)
  the two profiles are of different devices: /device:TPU:129 before, /device:TPU:127 now
where the time goes in v4:
time: 52.9 us
  Pallas kernels  52.2 us (99%)
  between operations  0.64 us (1%)
    pallas_call x1, Pallas kernels, body(): pl.pallas_call(functools.partial(soap_kernel, devices), out_shape=[pltpu....  50.2 us
    pallas_call x1, Pallas kernels, body(): pl.pallas_call(finish_kernel, out_shape=[jax.ShapeDtypeStruct((slots, wid...  2.05 us

profile of v4, /device:TPU:127, one launch (start us, length us, event | category | flops | bytes accessed | tf_op | source)
XLA Modules:
  0.0 52.9 jit_solution(15420356908000230484)
XLA Ops:
  0.6 50.2 %soap.1 = (f32[6,256,256]{2,1,0:T(8,128)S(1)}, f32[6,256,256]{2,1,0:T(8,128)S(1)}, s16[3,4,256,256]{3,2,1,0:T(8,128)(2,1)S(1)}, f32[3,2,2,2,256]{4,3,2,1,0:T(2,128)S(1)}) custom-call(s32[128]{0:T(128)} %starts_in.1, s32[384]{0:T(512)} %owners_in.1, bf16[1,4,256,256]{3,2,1,0:T(8,128)(2,1)} %grad.1, f32[6,256,256]{2,1,0:T(8,128)} %moment_in.1, ...), custom_call_target="tpu_custom_call" | custom-call | tf_op jit(solution)/shard_map/soap/pallas_call | solution.py:514
  50.8 2.1 %finish.1 = (f32[4,256,256]{2,1,0:T(8,128)}, f32[6,256,256]{2,1,0:T(8,128)}, f32[6,256,256]{2,1,0:T(8,128)}) custom-call(s16[3,4,256,256]{3,2,1,0:T(8,128)(2,1)S(1)} %get-tuple-element.7.codes, f32[3,2,2,2,256]{4,3,2,1,0:T(2,128)S(1)} %get-tuple-element.8.scales, f32[6,256,256]{2,1,0:T(8,128)S(1)} %get-tuple-element.9.first, ...), custom_call_target="tpu_custom_call" | custom-call | tf_op jit(solution)/shard_map/finish/pallas_call | solution.py:549

commit v5 on v4

--- a/solution.py
+++ b/solution.py
@@ -75,10 +75,9 @@
 
 def soap_kernel(
     devices, starts_in, owners_in, grad, moment_in, second_in, left_in, right_in, first_out, second_out, out, out_scales,
-    starts, owners, table, mine, theirs, other, gathered_a, gathered_b, moment, second, left, right, lt_high, lt_low, lh_high, lh_low, r_high, r_low,
+    starts, owners, table, mine, theirs, other, gathered_a, gathered_b, moment, second, left, right, lt_two, lh_two, r_high, r_low, rt_high, rt_low,
     base, update_a, update_b, scales_a, scales_b, second_late, codes, scales, far_in, far_scales, merged, merged_scales,
-    load_sem, swap_send, swap_recv, own_send, relay_send, ring_recv, hand_send, hand_recv, far_send, far_recv, near_send, near_recv, give_send, give_recv,
-    sf_send, sf_recv, sr_send, sr_recv, sh_send, sh_recv
+    load_sem, swap_sem, own_send, relay_send, ring_recv, hand_send, hand_recv, far_send, far_recv, near_send, near_recv, give_sem, scale_send, scale_recv
 ):
     me, core, right_peer, left_peer, twin = neighbours(devices)
     slots = grad.shape[1]
@@ -108,25 +107,23 @@
         load.start()
     greet(me, devices, right_peer, left_peer, twin)
 
-    def swap(w):
-        part = pl.ds(WAVE * w, WAVE)
-        return push(other.at[part], theirs.at[part], swap_send.at[w], swap_recv.at[w], twin)
+    swap = push(other, theirs, swap_sem.at[0], swap_sem.at[1], twin)
 
     def own(w, side, t):
         source = gathered[w].at[2, t, rows] if t is not None else gathered[w].at[2, :, rows]
         target = gathered[w].at[side["near"], t, rows] if t is not None else gathered[w].at[side["near"], :, rows]
-        arrived = ring_recv.at[side["near"], WAVE * w + (t or 0)]
+        arrived = ring_recv.at[side["at"], WAVE * w + (t or 0)]
         return push(source, target, own_send.at[side["at"], w], arrived, side["peer"])
 
     def relay(w, side, t):
         source = gathered[w].at[side["near"], t, rows] if t is not None else gathered[w].at[side["near"], :, rows]
         target = gathered[w].at[side["far"], t, rows] if t is not None else gathered[w].at[side["far"], :, rows]
-        arrived = ring_recv.at[side["far"], WAVE * w + (t or 0)]
+        arrived = ring_recv.at[2 + side["at"], WAVE * w + (t or 0)]
         return push(source, target, relay_send.at[side["at"], w], arrived, side["peer"])
 
-    def hand(w, k, t):
-        part = gathered[w].at[k, t, rows] if t is not None else gathered[w].at[k, :, rows]
-        return push(part, part, hand_send.at[w, k], hand_recv.at[w, k], twin)
+    def hand(w, k=None, t=None):
+        part = gathered[w].at[:, :, rows] if k is None else gathered[w].at[k, t, rows]
+        return push(part, part, hand_send.at[w], hand_recv.at[w], twin)
 
     to_right = dict(at=0, near=1, far=0, peer=right_peer, has=me >= 1, gives=me >= 2, sends=me < devices - 1, to_far=4, to_near=3)
     to_left = dict(at=1, near=3, far=4, peer=left_peer, has=me < devices - 1, gives=me < devices - 2, sends=me >= 1, to_far=0, to_near=1)
@@ -149,28 +146,21 @@
             def _():
                 relay(w, side, t).start()
 
-            @pl.when(side["has"])
-            def _():
-                hand(w, side["near"], t).start()
-
-    def add_up(w):
-        swap(w).wait_recv()
+            hand(w, side["near"], t).start()
+
+    loads[0].wait()
+    swap.start()
+    loads[1].wait()
+    swap.wait_recv()
+    for w in range(2):
         for t in range(WAVE):
             s = WAVE * w + t
             gathered[w][2, t, rows] = (mine[s].astype(F32) + theirs[s].astype(F32)).astype(BF16)
-
-    loads[0].wait()
-    swap(0).start()
-    swap(1).start()
-    loads[1].wait()
-    add_up(0)
-    for side in sides:
-        send_own(0, side)
-    for t in range(WAVE):
-        hand(0, 2, t).start()
-    add_up(1)
-    for t in range(WAVE):
-        hand(1, 2, t).start()
+        for side in sides:
+            send_own(w, side)
+    for w in range(2):
+        for t in range(WAVE):
+            hand(w, 2, t).start()
 
     for side in sides:
 
@@ -178,15 +168,15 @@
         def _():
             far_in[side["at"]] = jnp.zeros(far_in.shape[1:], I16)
             far_scales[side["at"]] = jnp.zeros(far_scales.shape[1:], F32)
-            out[side["at"]] = jnp.zeros(out.shape[1:], I16)
-            out_scales[side["at"]] = jnp.zeros(out_scales.shape[1:], F32)
-            for w in range(2):
-                gathered[w][side["near"]] = jnp.zeros(gathered[w].shape[1:], BF16)
+            out_scales[side["at"], core] = jnp.zeros(out_scales.shape[2:], F32)
+            for s in range(slots):
+                out[side["at"], s, rows] = jnp.zeros((half, out.shape[3]), I16)
+                gathered[s // WAVE][side["near"], s % WAVE, rows] = jnp.zeros((half, out.shape[3]), BF16)
 
         @pl.when(~side["gives"])
         def _():
-            for w in range(2):
-                gathered[w][side["far"]] = jnp.zeros(gathered[w].shape[1:], BF16)
+            for s in range(slots):
+                gathered[s // WAVE][side["far"], s % WAVE, rows] = jnp.zeros((half, out.shape[3]), BF16)
 
     loads[2].wait()
     loads[3].wait()
@@ -235,94 +225,70 @@
     loads[5].wait()
     loads[6].wait()
 
+    bias_one = 1.0 - BETA_ONE**STEP
+    bias_two = 1.0 - BETA_TWO**STEP
+    gain = bias_two**0.5 / bias_one
+
     def prepare(j):
         whole = left[j]
         l_two = split(whole.T)
+        h_two = split(left[j, rows])
         r_two = split(right[j])
-        h_two = split(left[j, rows])
-        lt_high[j], lt_low[j] = l_two
+        for at in range(2):
+            lt_two[j, at * whole.shape[0] : (at + 1) * whole.shape[0]] = l_two[at]
+            lh_two[j, at * half : (at + 1) * half] = h_two[at]
         r_high[j], r_low[j] = r_two
-        lh_high[j], lh_low[j] = h_two
+        rt_high[j], rt_low[j] = split(right[j].T)
         turned = dot_three(split(dot_three(l_two, split(moment[j]), NN)), r_two, NN)
-        base[j] = BETA_ONE * turned
-
-    place_in_plane = lax.rem(me, 16)
-    z_left, z_right = place_in_plane == 0, place_in_plane == 15
-    z_edge = z_left | z_right
-    x_left = (lax.rem(me, 4) == 0) & ~z_left
-
-    def middle(first_side, second_side):
-        for side in (first_side, second_side):
-            send_on(0, side)
-            send_own(1, side)
-
-    def middle_at_edge(early, late):
-        send_own(1, late)
-        send_on(0, early)
-        send_own(1, early)
-        send_on(1, early)
-        send_on(0, late)
-
-    @pl.loop(0, owned // 2)
+        base[j] = (BETA_ONE * gain) * turned
+
+    @pl.loop(0, owned)
     def _(j):
         prepare(j)
 
-    pl.when(z_left)(lambda: middle_at_edge(to_left, to_right))
-    pl.when(z_right)(lambda: middle_at_edge(to_right, to_left))
-    pl.when(x_left)(lambda: middle(to_left, to_right))
-    pl.when(~z_edge & ~x_left)(lambda: middle(to_right, to_left))
-
-    @pl.loop(owned // 2, owned)
-    def _(j):
-        prepare(j)
-
+    left_edge, right_edge = lax.rem(me, 4) == 0, lax.rem(me, 4) == 3
+
+    def in_order(step):
+        def each(order):
+            for w, side in order:
+                step(w, side)
+
+        pl.when(left_edge)(lambda: each(((0, to_left), (1, to_left), (0, to_right), (1, to_right))))
+        pl.when(right_edge)(lambda: each(((0, to_right), (1, to_right), (0, to_left), (1, to_left))))
+        pl.when(~(left_edge | right_edge))(lambda: each(((0, to_right), (0, to_left), (1, to_right), (1, to_left))))
+
+    in_order(send_on)
     loads[7].wait()
 
-    def arrive(w):
+    def pass_far(w):
         for t in range(WAVE):
             for side in sides:
-
-                @pl.when(side["gives"])
-                def _():
-                    relay(w, side, t).wait_recv()
-                    hand(w, side["far"], t).start()
-
-        hand(w, 2, None).wait_recv()
-        for side in sides:
-
-            @pl.when(side["has"])
-            def _():
-                hand(w, side["near"], None).wait_recv()
-
-            @pl.when(side["gives"])
-            def _():
-                hand(w, side["far"], None).wait_recv()
+                pl.when(side["gives"])(relay(w, side, t).wait_recv)
+                hand(w, side["far"], t).start()
+
+    def stacked(two, b_high, b_low, size):
+        full = dot(two, b_high, NN)
+        return full[:size] + (full[size:] + dot(two[:size], b_low, NN))
 
     def solve(j, gradient):
-        r_two = (r_high[j], r_low[j])
-        half_turned = dot(lt_high[j], gradient, NN) + dot(lt_low[j], gradient, NN)
-        turned = dot_three(split(half_turned), r_two, NN)
-        second_next = BETA_TWO * second[j] + (1.0 - BETA_TWO) * turned * turned
-        bias_one = 1.0 - BETA_ONE**STEP
-        bias_two = 1.0 - BETA_TWO**STEP
-        turned_moment = base[j] + (1.0 - BETA_ONE) * turned
-        scaled = turned_moment * (1.0 / bias_one) / (jnp.sqrt(second_next * (1.0 / bias_two)) + EPSILON)
-        new = dot_three(split(dot_three((lh_high[j], lh_low[j]), split(scaled), NN)), r_two, NT)
+        size = gradient.shape[0]
+        both = dot(lt_two[j], gradient, NN)
+        turned = stacked(jnp.concatenate(split(both[:size] + both[size:]), axis=0), r_high[j], r_low[j], size)
+        second_next = BETA_TWO * second[j] + ((1.0 - BETA_TWO) * turned) * turned
+        scaled = (base[j] + ((1.0 - BETA_ONE) * gain) * turned) / (second_next * lax.rsqrt(second_next) + EPSILON * bias_two**0.5)
+        s_high, s_low = split(scaled)
+        new = stacked(jnp.concatenate(split(stacked(lh_two[j], s_high, s_low, half)), axis=0), rt_high[j], rt_low[j], half)
         largest = jnp.maximum(jnp.max(jnp.abs(new), axis=0, keepdims=True), 1e-30)
         return second_next, jnp.round(new * (TOP / largest)).astype(jnp.int32).astype(I16), largest * (1.0 / TOP)
 
-    arrive(0)
+    pass_far(0)
+    hand(0).wait_recv()
 
     @pl.loop(0, owned // GROUP)
     def _(step):
-        @pl.when((step == 1) & ~z_left)
+        @pl.when(step == owned // GROUP - 1)
         def _():
-            pl.when(~z_right)(lambda: send_on(1, to_right))
-            send_on(1, to_left)
-
-        @pl.when((step == 1) & z_left)
-        def _():
-            send_on(1, to_right)
+            pass_far(1)
 
         for at in range(GROUP):
             j = step * GROUP + at
@@ -340,39 +306,40 @@
 
     def far(w, side, t):
         at = side["at"]
-        part = (at, w, t) if t is not None else (at, w)
-        return push(codes.at[part], far_in.at[part], far_send.at[at, w], far_recv.at[at, WAVE * w + (t or 0)], side["peer"])
-
-    def far_scale(w, side):
+        part = (at, w, t) if t is not None else (at,)
+        return push(codes.at[part], far_in.at[part], far_send.at[at], far_recv.at[at, WAVE * (w or 0) + (t or 0)], side["peer"])
+
+    def far_scale(side):
         at = side["at"]
-        return push(scales.at[at, w], far_scales.at[at, w], sf_send.at[at, w], sf_recv.at[at, w], side["peer"])
+        return push(scales.at[at], far_scales.at[at], scale_send.at[at], scale_recv.at[at], side["peer"])
 
     def near(w, side, t):
         at = side["at"]
-        part = (at, w, t) if t is not None else (at, w)
-        held = (at, WAVE * w + t, rows) if t is not None else (at, pl.ds(WAVE * w, WAVE), rows)
-        return push(merged.at[part], out.at[held], near_send.at[at, w], near_recv.at[at, WAVE * w + (t or 0)], side["peer"])
-
-    def near_scale(w, side):
+        part = (at, WAVE * w + t) if t is not None else (at,)
+        held = (at, WAVE * w + t, rows) if t is not None else (at, slice(None), rows)
+        return push(merged.at[part], out.at[held], near_send.at[at], near_recv.at[at, WAVE * (w or 0) + (t or 0)], side["peer"])
+
+    def near_scale(side):
         at = side["at"]
-        return push(merged_scales.at[at, w], out_scales.at[at, core, w], sr_send.at[at, w], sr_recv.at[at, w], side["peer"])
-
-    def give(k, s):
-        part = out.at[k, s, rows] if s is not None else out.at[k, :, rows]
-        return push(part, part, give_send.at[k], give_recv.at[k], twin)
-
-    def give_scale(k):
-        return push(out_scales.at[k, core], out_scales.at[k, core], sh_send.at[k], sh_recv.at[k], twin)
+        return push(merged_scales.at[at], out_scales.at[at, core], scale_send.at[2 + at], scale_recv.at[2 + at], side["peer"])
+
+    def give(k=None, s=None):
+        part = out.at[:, :, rows] if k is None else out.at[k, s, rows]
+        return push(part, part, give_sem.at[0], give_sem.at[1], twin)
+
+    def give_scale():
+        part = out_scales.at[:, core]
+        return push(part, part, scale_send.at[4], scale_recv.at[4], twin)
 
     def send_far(w):
         for t in range(WAVE):
             for side in sides:
                 codes[side["at"], w, t] = chosen(side["to_far"], WAVE * w + t, jnp.zeros((), I16))
                 pl.when(side["sends"])(far(w, side, t).start)
-        for side in sides:
-            for t in range(WAVE):
                 scales[side["at"], w, pl.ds(t, 1)] = chosen_scale(side["to_far"], WAVE * w + t, 0.0)
-            pl.when(side["sends"])(far_scale(w, side).start)
+        if w == 1:
+            for side in sides:
+                pl.when(side["sends"])(far_scale(side).start)
         for t in range(WAVE):
             s = WAVE * w + t
             out[2, s, rows] = chosen(2, s, jnp.zeros((), I16))
@@ -382,17 +349,17 @@
     def send_near(w, side):
         for t in range(WAVE):
             pl.when(side["has"])(far(w, side, t).wait_recv)
-            merged[side["at"], w, t] = chosen(side["to_near"], WAVE * w + t, far_in[side["at"], w, t])
+            merged[side["at"], WAVE * w + t] = chosen(side["to_near"], WAVE * w + t, far_in[side["at"], w, t])
             pl.when(side["sends"])(near(w, side, t).start)
-        pl.when(side["has"])(far_scale(w, side).wait_recv)
-        for t in range(WAVE):
-            merged_scales[side["at"], w, pl.ds(t, 1)] = chosen_scale(
-                side["to_near"], WAVE * w + t, far_scales[side["at"], w, pl.ds(t, 1)]
-            )
-        pl.when(side["sends"])(near_scale(w, side).start)
+        if w == 1:
+            pl.when(side["has"])(far_scale(side).wait_recv)
+            for s in range(slots):
+                place = (side["at"], s // WAVE, pl.ds(s % WAVE, 1))
+                merged_scales[place] = chosen_scale(side["to_near"], s, far_scales[place])
+            pl.when(side["sends"])(near_scale(side).start)
 
     send_far(0)
-    arrive(1)
+    hand(1).wait_recv()
 
     @pl.loop(0, LATE // GROUP)
     def _(step):
@@ -402,16 +369,7 @@
             second_late[b], update_b[b], scales_b[b] = solve(j, gathered_b[table[2, j], table[3, j]])
 
     send_far(1)
-    give_scale(2).start()
-
-    def send_all_near(order):
-        for w, side in order:
-            send_near(w, side)
-
-    pl.when(z_left)(lambda: send_all_near(((0, to_left), (1, to_left), (0, to_right), (1, to_right))))
-    pl.when(z_right)(lambda: send_all_near(((0, to_right), (1, to_right), (0, to_left), (1, to_left))))
-    pl.when(x_left)(lambda: send_all_near(((0, to_left), (0, to_right), (1, to_left), (1, to_right))))
-    pl.when(~z_edge & ~x_left)(lambda: send_all_near(((0, to_right), (0, to_left), (1, to_right), (1, to_left))))
+    in_order(send_near)
 
     @pl.loop(0, owned)
     def _(j):
@@ -422,69 +380,44 @@
 
     for s in range(slots):
         for side in sides:
-
-            @pl.when(side["has"])
-            def _():
-                near(s // WAVE, side, s % WAVE).wait_recv()
-                give(side["at"], s).start()
-
+            pl.when(side["has"])(near(s // WAVE, side, s % WAVE).wait_recv)
+            give(side["at"], s).start()
     for side in sides:
-
-        @pl.when(side["has"])
-        def _():
-            for w in range(2):
-                near_scale(w, side).wait_recv()
-            give_scale(side["at"]).start()
-
+        pl.when(side["has"])(near_scale(side).wait_recv)
+    give_scale().start()
+
+    swap.wait_send()
     for w in range(2):
-        swap(w).wait_send()
-        hand(w, 2, None).wait_send()
-    give(2, None).wait_send()
-    give_scale(2).wait_send()
+        hand(w).wait_send()
     for side in sides:
 
         @pl.when(side["sends"])
         def _():
             for w in range(2):
                 own(w, side, None).wait_send()
-                far(w, side, None).wait_send()
-                far_scale(w, side).wait_send()
-                near(w, side, None).wait_send()
-                near_scale(w, side).wait_send()
+            far(None, side, None).wait_send()
+            far_scale(side).wait_send()
+            near(None, side, None).wait_send()
+            near_scale(side).wait_send()
 
         @pl.when(side["has"] & side["sends"])
         def _():
             for w in range(2):
                 relay(w, side, None).wait_send()
 
-        @pl.when(side["has"])
-        def _():
-            for w in range(2):
-                hand(w, side["near"], None).wait_send()
-            give(side["at"], None).wait_send()
-            give_scale(side["at"]).wait_send()
-
-        @pl.when(side["gives"])
-        def _():
-            for w in range(2):
-                hand(w, side["far"], None).wait_send()
-
-    give(2, None).wait_recv()
-    give_scale(2).wait_recv()
-    for side in sides:
-
-        @pl.when(side["has"])
-        def _():
-            give(side["at"], None).wait_recv()
-            give_scale(side["at"]).wait_recv()
+    give().wait_send()
+    give_scale().wait_send()
+    give().wait_recv()
+    give_scale().wait_recv()
 
 
 def finish_kernel(codes, scales, first, second, direction, first_new, second_new, decoded, sem):
     slots = codes.shape[1]
     half = codes.shape[2] // 2
     copies = [pltpu.make_async_copy(first, first_new, sem.at[0]), pltpu.make_async_copy(second, second_new, sem.at[1])]
-    for copy in copies:
-        copy.start()
+    for j in range(first.shape[0]):
+        pltpu.make_async_copy(first.at[j], first_new.at[j], sem.at[0]).start()
+        pltpu.make_async_copy(second.at[j], second_new.at[j], sem.at[1]).start()
     for s in range(slots):
         for core in range(2):
             rows = pl.ds(core * half, half)
@@ -528,18 +461,20 @@
             *[pltpu.VMEM((slots, half, width), BF16)] * 3,
             *[pltpu.VMEM((5, WAVE, width, width), BF16)] * 2,
             *[pltpu.VMEM(matrices, F32)] * 4,
-            *[pltpu.VMEM(matrices, BF16)] * 2,
-            *[pltpu.VMEM(halves, BF16)] * 2,
-            *[pltpu.VMEM(matrices, BF16)] * 2,
+            pltpu.VMEM((owned, 2 * width, width), BF16),
+            pltpu.VMEM((owned, width, width), BF16),
+            *[pltpu.VMEM(matrices, BF16)] * 4,
             pltpu.VMEM(matrices, F32),
             pltpu.VMEM(halves, I16),
             pltpu.VMEM((LATE, half, width), I16),
             pltpu.VMEM((owned, 1, width), F32),
             pltpu.VMEM((LATE, 1, width), F32),
             pltpu.VMEM((LATE, width, width), F32),
-            *[pltpu.VMEM((2, 2, WAVE, half, width), I16), pltpu.VMEM((2, 2, WAVE, width), F32)] * 3,
-            dma((8,)), *[dma((2,))] * 2, *[dma((2, 2))] * 2, dma((5, slots)), *[dma((2, 5))] * 2,
-            *[dma((2, 2)), dma((2, slots))] * 2, *[dma((3,))] * 2, *[dma((2, 2))] * 4, *[dma((3,))] * 2,
+            *[pltpu.VMEM((2, 2, WAVE, half, width), I16), pltpu.VMEM((2, 2, WAVE, width), F32)] * 2,
+            pltpu.VMEM((2, slots, half, width), I16),
+            pltpu.VMEM((2, 2, WAVE, width), F32),
+            dma((8,)), dma((2,)), *[dma((2, 2))] * 2, dma((4, slots)), *[dma((2,))] * 2,
+            *[dma((2,)), dma((2, slots))] * 2, dma((2,)), *[dma((5,))] * 2,
         ],
         compiler_params=pltpu.CompilerParams(collective_id=0, has_side_effects=True, vmem_limit_bytes=ROOM),
         name="soap",

time: 52.9 us -> 46.9 us (0.89)
  the two profiles are of different devices: /device:TPU:127 before, /device:TPU:129 now
where the time goes in v5:
time: 46.9 us; the launch traced here: 46.8 us
  Pallas kernels  46.1 us (98%)
  between operations  0.64 us (1%)
    pallas_call x1, Pallas kernels, body(): pl.pallas_call(functools.partial(soap_kernel, devices), out_shape=[pltpu....  44.1 us
    pallas_call x1, Pallas kernels, body(): pl.pallas_call(finish_kernel, out_shape=[jax.ShapeDtypeStruct((slots, wid...  2.05 us

profile of v5, /device:TPU:129, one launch (start us, length us, event | category | flops | bytes accessed | tf_op | source)
XLA Modules:
  0.0 46.8 jit_solution(12307409890767499697)
XLA Ops:
  0.6 44.1 %soap.1 = (f32[6,256,256]{2,1,0:T(8,128)S(1)}, f32[6,256,256]{2,1,0:T(8,128)S(1)}, s16[3,4,256,256]{3,2,1,0:T(8,128)(2,1)S(1)}, f32[3,2,2,2,256]{4,3,2,1,0:T(2,128)S(1)}) custom-call(s32[128]{0:T(128)} %starts_in.1, s32[384]{0:T(512)} %owners_in.1, bf16[1,4,256,256]{3,2,1,0:T(8,128)(2,1)} %grad.1, f32[6,256,256]{2,1,0:T(8,128)} %moment_in.1, ...), custom_call_target="tpu_custom_call" | custom-call | tf_op jit(solution)/shard_map/soap/pallas_call | solution.py:447
  44.7 2.0 %finish.1 = (f32[4,256,256]{2,1,0:T(8,128)}, f32[6,256,256]{2,1,0:T(8,128)}, f32[6,256,256]{2,1,0:T(8,128)}) custom-call(s16[3,4,256,256]{3,2,1,0:T(8,128)(2,1)S(1)} %get-tuple-element.7.codes, f32[3,2,2,2,256]{4,3,2,1,0:T(2,128)S(1)} %get-tuple-element.8.scales, f32[6,256,256]{2,1,0:T(8,128)S(1)} %get-tuple-element.9.first, ...), custom_call_target="tpu_custom_call" | custom-call | tf_op jit(solution)/shard_map/finish/pallas_call | solution.py:484

commit v6 on v5

--- a/solution.py
+++ b/solution.py
@@ -68,7 +68,6 @@
 
 NN = ((1,), (0,))
 NT = ((1,), (1,))
-GROUP = 2
 WAVE = 2
 LATE = 4
 
@@ -76,7 +75,7 @@
 def soap_kernel(
     devices, starts_in, owners_in, grad, moment_in, second_in, left_in, right_in, first_out, second_out, out, out_scales,
     starts, owners, table, mine, theirs, other, gathered_a, gathered_b, moment, second, left, right, lt_two, lh_two, r_high, r_low, rt_high, rt_low,
-    base, update_a, update_b, scales_a, scales_b, second_late, codes, scales, far_in, far_scales, merged, merged_scales,
+    base, update_a, update_b, scales_a, scales_b, second_late, codes, scales, far_in, far_scales, merged, merged_scales, h_two, s_high, s_low, z_two,
     load_sem, swap_sem, own_send, relay_send, ring_recv, hand_send, hand_recv, far_send, far_recv, near_send, near_recv, give_sem, scale_send, scale_recv
 ):
     me, core, right_peer, left_peer, twin = neighbours(devices)
@@ -107,7 +106,8 @@
         load.start()
     greet(me, devices, right_peer, left_peer, twin)
 
-    swap = push(other, theirs, swap_sem.at[0], swap_sem.at[1], twin)
+    def swap(s):
+        return push(other.at[s], theirs.at[s], swap_sem.at[0, s], swap_sem.at[1, s], twin)
 
     def own(w, side, t):
         source = gathered[w].at[2, t, rows] if t is not None else gathered[w].at[2, :, rows]
@@ -129,11 +129,8 @@
     to_left = dict(at=1, near=3, far=4, peer=left_peer, has=me < devices - 1, gives=me < devices - 2, sends=me >= 1, to_far=0, to_near=1)
     sides = (to_right, to_left)
 
-    def send_own(w, side):
-        @pl.when(side["sends"])
-        def _():
-            for t in range(WAVE):
-                own(w, side, t).start()
+    def send_own(w, side, t):
+        pl.when(side["sends"])(own(w, side, t).start)
 
     def send_on(w, side):
         for t in range(WAVE):
@@ -149,15 +146,16 @@
             hand(w, side["near"], t).start()
 
     loads[0].wait()
-    swap.start()
+    for s in range(slots):
+        swap(s).start()
     loads[1].wait()
-    swap.wait_recv()
     for w in range(2):
         for t in range(WAVE):
             s = WAVE * w + t
+            swap(s).wait_recv()
             gathered[w][2, t, rows] = (mine[s].astype(F32) + theirs[s].astype(F32)).astype(BF16)
-        for side in sides:
-            send_own(w, side)
+            for side in sides:
+                send_own(w, side, t)
     for w in range(2):
         for t in range(WAVE):
             hand(w, 2, t).start()
@@ -232,11 +230,11 @@
     def prepare(j):
         whole = left[j]
         l_two = split(whole.T)
-        h_two = split(left[j, rows])
+        half_l = split(left[j, rows])
         r_two = split(right[j])
         for at in range(2):
             lt_two[j, at * whole.shape[0] : (at + 1) * whole.shape[0]] = l_two[at]
-            lh_two[j, at * half : (at + 1) * half] = h_two[at]
+            lh_two[j, at * half : (at + 1) * half] = half_l[at]
         r_high[j], r_low[j] = r_two
         rt_high[j], rt_low[j] = split(right[j].T)
         turned = dot_three(split(dot_three(l_two, split(moment[j]), NN)), r_two, NN)
@@ -266,33 +264,38 @@
                 pl.when(side["gives"])(relay(w, side, t).wait_recv)
                 hand(w, side["far"], t).start()
 
-    def stacked(two, b_high, b_low, size):
+    def stacked(two, b_high, b_low):
+        size = two.shape[0] // 2
         full = dot(two, b_high, NN)
         return full[:size] + (full[size:] + dot(two[:size], b_low, NN))
 
-    def solve(j, gradient):
-        size = gradient.shape[0]
-        both = dot(lt_two[j], gradient, NN)
-        turned = stacked(jnp.concatenate(split(both[:size] + both[size:]), axis=0), r_high[j], r_low[j], size)
-        second_next = BETA_TWO * second[j] + ((1.0 - BETA_TWO) * turned) * turned
-        scaled = (base[j] + ((1.0 - BETA_ONE) * gain) * turned) / (second_next * lax.rsqrt(second_next) + EPSILON * bias_two**0.5)
-        s_high, s_low = split(scaled)
-        new = stacked(jnp.concatenate(split(stacked(lh_two[j], s_high, s_low, half)), axis=0), rt_high[j], rt_low[j], half)
-        largest = jnp.maximum(jnp.max(jnp.abs(new), axis=0, keepdims=True), 1e-30)
-        return second_next, jnp.round(new * (TOP / largest)).astype(jnp.int32).astype(I16), largest * (1.0 / TOP)
+    def stack(two, at, value):
+        size = value.shape[0]
+        two[at, :size], two[at, size:] = split(value)
+
+    def solve(indices, source, second_to, update_to, scales_to, between):
+        size = source.shape[2]
+        for at, j in enumerate(indices):
+            both = dot(lt_two[j], source[table[2, j], table[3, j]], NN)
+            stack(h_two, at, both[:size] + both[size:])
+        for at, j in enumerate(indices):
+            turned = stacked(h_two[at], r_high[j], r_low[j])
+            second_next = BETA_TWO * second[j] + ((1.0 - BETA_TWO) * turned) * turned
+            second_to[at] = second_next
+            scaled = (base[j] + ((1.0 - BETA_ONE) * gain) * turned) / (second_next * lax.rsqrt(second_next) + EPSILON * bias_two**0.5)
+            s_high[at], s_low[at] = split(scaled)
+        between()
+        for at, j in enumerate(indices):
+            stack(z_two, at, stacked(lh_two[j], s_high[at], s_low[at]))
+        for at, j in enumerate(indices):
+            new = stacked(z_two[at], rt_high[j], rt_low[j])
+            largest = jnp.maximum(jnp.max(jnp.abs(new), axis=0, keepdims=True), 1e-30)
+            update_to[at] = jnp.round(new * (TOP / largest)).astype(jnp.int32).astype(I16)
+            scales_to[at] = largest * (1.0 / TOP)
 
     pass_far(0)
     hand(0).wait_recv()
-
-    @pl.loop(0, owned // GROUP)
-    def _(step):
-        @pl.when(step == owned // GROUP - 1)
-        def _():
-            pass_far(1)
-
-        for at in range(GROUP):
-            j = step * GROUP + at
-            second_out[j], update_a[j], scales_a[j] = solve(j, gathered_a[table[2, j], table[3, j]])
+    solve(range(owned), gathered_a, second_out, update_a, scales_a, lambda: pass_far(1))
 
     def chosen(k, s, absent):
         at = table[7 + 2 * k, s]
@@ -361,12 +364,7 @@
     send_far(0)
     hand(1).wait_recv()
 
-    @pl.loop(0, LATE // GROUP)
-    def _(step):
-        for at in range(GROUP):
-            b = step * GROUP + at
-            j = table[5, b]
-            second_late[b], update_b[b], scales_b[b] = solve(j, gathered_b[table[2, j], table[3, j]])
+    solve([table[5, b] for b in range(LATE)], gathered_b, second_late, update_b, scales_b, lambda: None)
 
     send_far(1)
     in_order(send_near)
@@ -386,7 +384,8 @@
         pl.when(side["has"])(near_scale(side).wait_recv)
     give_scale().start()
 
-    swap.wait_send()
+    for s in range(slots):
+        swap(s).wait_send()
     for w in range(2):
         hand(w).wait_send()
     for side in sides:
@@ -473,7 +472,10 @@
             *[pltpu.VMEM((2, 2, WAVE, half, width), I16), pltpu.VMEM((2, 2, WAVE, width), F32)] * 2,
             pltpu.VMEM((2, slots, half, width), I16),
             pltpu.VMEM((2, 2, WAVE, width), F32),
-            dma((8,)), dma((2,)), *[dma((2, 2))] * 2, dma((4, slots)), *[dma((2,))] * 2,
+            pltpu.VMEM((owned, 2 * width, width), BF16),
+            *[pltpu.VMEM(matrices, BF16)] * 2,
+            pltpu.VMEM((owned, width, width), BF16),
+            dma((8,)), dma((2, slots)), *[dma((2, 2))] * 2, dma((4, slots)), *[dma((2,))] * 2,
             *[dma((2,)), dma((2, slots))] * 2, dma((2,)), *[dma((5,))] * 2,
         ],
         compiler_params=pltpu.CompilerParams(collective_id=0, has_side_effects=True, vmem_limit_bytes=ROOM),

time: 46.9 us -> 43.3 us (0.923)
  Pallas kernels: 46.1 us -> 42.6 us
    pallas_call x1, Pallas kernels: 44.1 us -> 40.6 us  [body(): pl.pallas_call(functools.partial(soap_kernel, devices), out_shape=[pltpu....]
where the time goes in v6:
time: 43.3 us
  Pallas kernels  42.6 us (98%)
  between operations  0.64 us (1%)
    pallas_call x1, Pallas kernels, body(): pl.pallas_call(functools.partial(soap_kernel, devices), out_shape=[pltpu....  40.6 us
    pallas_call x1, Pallas kernels, body(): pl.pallas_call(finish_kernel, out_shape=[jax.ShapeDtypeStruct((slots, wid...  2.05 us

profile of v6, /device:TPU:129, one launch (start us, length us, event | category | flops | bytes accessed | tf_op | source)
XLA Modules:
  0.0 43.3 jit_solution(8378931112519496379)
XLA Ops:
  0.6 40.6 %soap.1 = (f32[6,256,256]{2,1,0:T(8,128)S(1)}, f32[6,256,256]{2,1,0:T(8,128)S(1)}, s16[3,4,256,256]{3,2,1,0:T(8,128)(2,1)S(1)}, f32[3,2,2,2,256]{4,3,2,1,0:T(2,128)S(1)}) custom-call(s32[128]{0:T(128)} %starts_in.1, s32[384]{0:T(512)} %owners_in.1, bf16[1,4,256,256]{3,2,1,0:T(8,128)(2,1)} %grad.1, f32[6,256,256]{2,1,0:T(8,128)} %moment_in.1, ...), custom_call_target="tpu_custom_call" | custom-call | tf_op jit(solution)/shard_map/soap/pallas_call | solution.py:446
  41.2 2.0 %finish.1 = (f32[4,256,256]{2,1,0:T(8,128)}, f32[6,256,256]{2,1,0:T(8,128)}, f32[6,256,256]{2,1,0:T(8,128)}) custom-call(s16[3,4,256,256]{3,2,1,0:T(8,128)(2,1)S(1)} %get-tuple-element.7.codes, f32[3,2,2,2,256]{4,3,2,1,0:T(2,128)S(1)} %get-tuple-element.8.scales, f32[6,256,256]{2,1,0:T(8,128)S(1)} %get-tuple-element.9.first, ...), custom_call_target="tpu_custom_call" | custom-call | tf_op jit(solution)/shard_map/finish/pallas_call | solution.py:486

commit v7 on v6

--- a/solution.py
+++ b/solution.py
@@ -132,8 +132,8 @@
     def send_own(w, side, t):
         pl.when(side["sends"])(own(w, side, t).start)
 
-    def send_on(w, side):
-        for t in range(WAVE):
+    def send_on(w, side, places=range(WAVE)):
+        for t in places:
 
             @pl.when(side["has"])
             def _():
@@ -144,6 +144,12 @@
                 relay(w, side, t).start()
 
             hand(w, side["near"], t).start()
+
+    left_edge, right_edge = lax.rem(me, 4) == 0, lax.rem(me, 4) == 3
+    z_edge = (lax.rem(me, 16) == 0) | (lax.rem(me, 16) == 15)
+    after_edge = (lax.rem(me, 16) == 1) | (lax.rem(me, 16) == 14)
+    to_right["late"] = left_edge | (lax.rem(me, 16) == 1)
+    to_left["late"] = right_edge | (lax.rem(me, 16) == 14)
 
     loads[0].wait()
     for s in range(slots):
@@ -155,7 +161,12 @@
             swap(s).wait_recv()
             gathered[w][2, t, rows] = (mine[s].astype(F32) + theirs[s].astype(F32)).astype(BF16)
             for side in sides:
-                send_own(w, side, t)
+                if w == 0:
+                    send_own(w, side, t)
+                elif t == 0:
+                    pl.when(side["late"] | ~z_edge)(functools.partial(send_own, w, side, t))
+                else:
+                    pl.when(side["late"])(functools.partial(send_own, w, side, t))
     for w in range(2):
         for t in range(WAVE):
             hand(w, 2, t).start()
@@ -240,23 +251,38 @@
         turned = dot_three(split(dot_three(l_two, split(moment[j]), NN)), r_two, NN)
         base[j] = (BETA_ONE * gain) * turned
 
-    @pl.loop(0, owned)
+    @pl.loop(0, owned // 2)
     def _(j):
         prepare(j)
 
-    left_edge, right_edge = lax.rem(me, 4) == 0, lax.rem(me, 4) == 3
-
-    def in_order(step):
-        def each(order):
-            for w, side in order:
-                step(w, side)
-
-        pl.when(left_edge)(lambda: each(((0, to_left), (1, to_left), (0, to_right), (1, to_right))))
-        pl.when(right_edge)(lambda: each(((0, to_right), (1, to_right), (0, to_left), (1, to_left))))
-        pl.when(~(left_edge | right_edge))(lambda: each(((0, to_right), (0, to_left), (1, to_right), (1, to_left))))
-
-    in_order(send_on)
-    loads[7].wait()
+    for side in sides:
+
+        @pl.when(~side["late"])
+        def _():
+            send_on(0, side)
+            pl.when(z_edge)(functools.partial(send_own, 1, side, 0))
+            send_own(1, side, 1)
+
+    @pl.loop(owned // 2, owned)
+    def _(j):
+        prepare(j)
+
+    for side in sides:
+
+        @pl.when(side["late"])
+        def _():
+            send_on(0, side)
+
+    def send_on_late_wave(late, places, where):
+        for side in sides:
+
+            @pl.when((side["late"] == late) & where)
+            def _():
+                send_on(1, side, places)
+
+    send_on_late_wave(False, (0,), me >= 0)
+    send_on_late_wave(False, (1,), z_edge)
+    send_on_late_wave(True, (0, 1), after_edge)
 
     def pass_far(w):
         for t in range(WAVE):
@@ -293,9 +319,12 @@
             update_to[at] = jnp.round(new * (TOP / largest)).astype(jnp.int32).astype(I16)
             scales_to[at] = largest * (1.0 / TOP)
 
+    loads[7].wait()
     pass_far(0)
+    send_on_late_wave(False, (1,), ~z_edge)
+    send_on_late_wave(True, (0,), ~after_edge)
     hand(0).wait_recv()
-    solve(range(owned), gathered_a, second_out, update_a, scales_a, lambda: pass_far(1))
+    solve(range(owned), gathered_a, second_out, update_a, scales_a, lambda: send_on_late_wave(True, (1,), ~after_edge))
 
     def chosen(k, s, absent):
         at = table[7 + 2 * k, s]
@@ -362,12 +391,19 @@
             pl.when(side["sends"])(near_scale(side).start)
 
     send_far(0)
+    pass_far(1)
     hand(1).wait_recv()
 
     solve([table[5, b] for b in range(LATE)], gathered_b, second_late, update_b, scales_b, lambda: None)
 
     send_far(1)
-    in_order(send_near)
+    def each(order):
+        for w, side in order:
+            send_near(w, side)
+
+    pl.when(left_edge)(lambda: each(((0, to_left), (1, to_left), (0, to_right), (1, to_right))))
+    pl.when(right_edge)(lambda: each(((0, to_right), (1, to_right), (0, to_left), (1, to_left))))
+    pl.when(~(left_edge | right_edge))(lambda: each(((0, to_right), (0, to_left), (1, to_right), (1, to_left))))
 
     @pl.loop(0, owned)
     def _(j):

time: 43.3 us -> 42.6 us (0.984)
  Pallas kernels: 42.6 us -> 41.8 us
    pallas_call x1, Pallas kernels: 40.6 us -> 39.8 us  [body(): pl.pallas_call(functools.partial(soap_kernel, devices), out_shape=[pltpu....]
where the time goes in v7:
time: 42.6 us; the launch traced here: 42.5 us
  Pallas kernels  41.8 us (98%)
  between operations  0.64 us (2%)
    pallas_call x1, Pallas kernels, body(): pl.pallas_call(functools.partial(soap_kernel, devices), out_shape=[pltpu....  39.8 us
    pallas_call x1, Pallas kernels, body(): pl.pallas_call(finish_kernel, out_shape=[jax.ShapeDtypeStruct((slots, wid...  2.05 us

profile of v7, /device:TPU:129, one launch (start us, length us, event | category | flops | bytes accessed | tf_op | source)
XLA Modules:
  0.0 42.5 jit_solution(8580742140249372785)
XLA Ops:
  0.6 39.8 %soap.1 = (f32[6,256,256]{2,1,0:T(8,128)S(1)}, f32[6,256,256]{2,1,0:T(8,128)S(1)}, s16[3,4,256,256]{3,2,1,0:T(8,128)(2,1)S(1)}, f32[3,2,2,2,256]{4,3,2,1,0:T(2,128)S(1)}) custom-call(s32[128]{0:T(128)} %starts_in.1, s32[384]{0:T(512)} %owners_in.1, bf16[1,4,256,256]{3,2,1,0:T(8,128)(2,1)} %grad.1, f32[6,256,256]{2,1,0:T(8,128)} %moment_in.1, ...), custom_call_target="tpu_custom_call" | custom-call | tf_op jit(solution)/shard_map/soap/pallas_call | solution.py:482
  40.4 2.0 %finish.1 = (f32[4,256,256]{2,1,0:T(8,128)}, f32[6,256,256]{2,1,0:T(8,128)}, f32[6,256,256]{2,1,0:T(8,128)}) custom-call(s16[3,4,256,256]{3,2,1,0:T(8,128)(2,1)S(1)} %get-tuple-element.7.codes, f32[3,2,2,2,256]{4,3,2,1,0:T(2,128)S(1)} %get-tuple-element.8.scales, f32[6,256,256]{2,1,0:T(8,128)S(1)} %get-tuple-element.9.first, ...), custom_call_target="tpu_custom_call" | custom-call | tf_op jit(solution)/shard_map/finish/pallas_call | solution.py:522

commit v8 on v7

--- a/solution.py
+++ b/solution.py
@@ -401,8 +401,8 @@
         for w, side in order:
             send_near(w, side)
 
-    pl.when(left_edge)(lambda: each(((0, to_left), (1, to_left), (0, to_right), (1, to_right))))
-    pl.when(right_edge)(lambda: each(((0, to_right), (1, to_right), (0, to_left), (1, to_left))))
+    pl.when(left_edge)(lambda: each(((0, to_left), (0, to_right), (1, to_left), (1, to_right))))
+    pl.when(right_edge)(lambda: each(((0, to_right), (0, to_left), (1, to_right), (1, to_left))))
     pl.when(~(left_edge | right_edge))(lambda: each(((0, to_right), (0, to_left), (1, to_right), (1, to_left))))
 
     @pl.loop(0, owned)

time: 42.6 us -> 42.6 us (level)
  no operation moved by 1% of the time
where the time goes in v8:
time: 42.6 us; the launch traced here: 42.5 us
  Pallas kernels  41.8 us (98%)
  between operations  0.64 us (2%)
    pallas_call x1, Pallas kernels, body(): pl.pallas_call(functools.partial(soap_kernel, devices), out_shape=[pltpu....  39.8 us
    pallas_call x1, Pallas kernels, body(): pl.pallas_call(finish_kernel, out_shape=[jax.ShapeDtypeStruct((slots, wid...  2.05 us

profile of v8, /device:TPU:129, one launch (start us, length us, event | category | flops | bytes accessed | tf_op | source)
XLA Modules:
  0.0 42.5 jit_solution(17425105167980181097)
XLA Ops:
  0.6 39.8 %soap.1 = (f32[6,256,256]{2,1,0:T(8,128)S(1)}, f32[6,256,256]{2,1,0:T(8,128)S(1)}, s16[3,4,256,256]{3,2,1,0:T(8,128)(2,1)S(1)}, f32[3,2,2,2,256]{4,3,2,1,0:T(2,128)S(1)}) custom-call(s32[128]{0:T(128)} %starts_in.1, s32[384]{0:T(512)} %owners_in.1, bf16[1,4,256,256]{3,2,1,0:T(8,128)(2,1)} %grad.1, f32[6,256,256]{2,1,0:T(8,128)} %moment_in.1, ...), custom_call_target="tpu_custom_call" | custom-call | tf_op jit(solution)/shard_map/soap/pallas_call | solution.py:482
  40.4 2.0 %finish.1 = (f32[4,256,256]{2,1,0:T(8,128)}, f32[6,256,256]{2,1,0:T(8,128)}, f32[6,256,256]{2,1,0:T(8,128)}) custom-call(s16[3,4,256,256]{3,2,1,0:T(8,128)(2,1)S(1)} %get-tuple-element.7.codes, f32[3,2,2,2,256]{4,3,2,1,0:T(2,128)S(1)} %get-tuple-element.8.scales, f32[6,256,256]{2,1,0:T(8,128)S(1)} %get-tuple-element.9.first, ...), custom_call_target="tpu_custom_call" | custom-call | tf_op jit(solution)/shard_map/finish/pallas_call | solution.py:522

commit v9 on v8

--- a/solution.py
+++ b/solution.py
@@ -366,29 +366,31 @@
     def send_far(w):
         for t in range(WAVE):
             for side in sides:
-                codes[side["at"], w, t] = chosen(side["to_far"], WAVE * w + t, jnp.zeros((), I16))
-                pl.when(side["sends"])(far(w, side, t).start)
                 scales[side["at"], w, pl.ds(t, 1)] = chosen_scale(side["to_far"], WAVE * w + t, 0.0)
         if w == 1:
             for side in sides:
                 pl.when(side["sends"])(far_scale(side).start)
         for t in range(WAVE):
+            for side in sides:
+                codes[side["at"], w, t] = chosen(side["to_far"], WAVE * w + t, jnp.zeros((), I16))
+                pl.when(side["sends"])(far(w, side, t).start)
+        for t in range(WAVE):
             s = WAVE * w + t
             out[2, s, rows] = chosen(2, s, jnp.zeros((), I16))
             give(2, s).start()
             out_scales[2, core, w, pl.ds(t, 1)] = chosen_scale(2, s, 0.0)
 
     def send_near(w, side):
-        for t in range(WAVE):
-            pl.when(side["has"])(far(w, side, t).wait_recv)
-            merged[side["at"], WAVE * w + t] = chosen(side["to_near"], WAVE * w + t, far_in[side["at"], w, t])
-            pl.when(side["sends"])(near(w, side, t).start)
         if w == 1:
             pl.when(side["has"])(far_scale(side).wait_recv)
             for s in range(slots):
                 place = (side["at"], s // WAVE, pl.ds(s % WAVE, 1))
                 merged_scales[place] = chosen_scale(side["to_near"], s, far_scales[place])
             pl.when(side["sends"])(near_scale(side).start)
+        for t in range(WAVE):
+            pl.when(side["has"])(far(w, side, t).wait_recv)
+            merged[side["at"], WAVE * w + t] = chosen(side["to_near"], WAVE * w + t, far_in[side["at"], w, t])
+            pl.when(side["sends"])(near(w, side, t).start)
 
     send_far(0)
     pass_far(1)
@@ -413,12 +415,13 @@
         second_out[j] = jnp.where(late, second_late[table[4, j]], jnp.where(early, second_out[j], 0.0))
 
     for s in range(slots):
+        if s == slots - 1:
+            for side in sides:
+                pl.when(side["has"])(near_scale(side).wait_recv)
+            give_scale().start()
         for side in sides:
             pl.when(side["has"])(near(s // WAVE, side, s % WAVE).wait_recv)
             give(side["at"], s).start()
-    for side in sides:
-        pl.when(side["has"])(near_scale(side).wait_recv)
-    give_scale().start()
 
     for s in range(slots):
         swap(s).wait_send()

time: 42.6 us -> 42.6 us (level)
  no operation moved by 1% of the time
where the time goes in v9:
time: 42.6 us; the launch traced here: 42.5 us
  Pallas kernels  41.9 us (98%)
  between operations  0.64 us (2%)
    pallas_call x1, Pallas kernels, body(): pl.pallas_call(functools.partial(soap_kernel, devices), out_shape=[pltpu....  39.8 us
    pallas_call x1, Pallas kernels, body(): pl.pallas_call(finish_kernel, out_shape=[jax.ShapeDtypeStruct((slots, wid...  2.05 us

profile of v9, /device:TPU:129, one launch (start us, length us, event | category | flops | bytes accessed | tf_op | source)
XLA Modules:
  0.0 42.5 jit_solution(6127936153614390987)
XLA Ops:
  0.6 39.8 %soap.1 = (f32[6,256,256]{2,1,0:T(8,128)S(1)}, f32[6,256,256]{2,1,0:T(8,128)S(1)}, s16[3,4,256,256]{3,2,1,0:T(8,128)(2,1)S(1)}, f32[3,2,2,2,256]{4,3,2,1,0:T(2,128)S(1)}) custom-call(s32[128]{0:T(128)} %starts_in.1, s32[384]{0:T(512)} %owners_in.1, bf16[1,4,256,256]{3,2,1,0:T(8,128)(2,1)} %grad.1, f32[6,256,256]{2,1,0:T(8,128)} %moment_in.1, ...), custom_call_target="tpu_custom_call" | custom-call | tf_op jit(solution)/shard_map/soap/pallas_call | solution.py:485
  40.5 2.0 %finish.1 = (f32[4,256,256]{2,1,0:T(8,128)}, f32[6,256,256]{2,1,0:T(8,128)}, f32[6,256,256]{2,1,0:T(8,128)}) custom-call(s16[3,4,256,256]{3,2,1,0:T(8,128)(2,1)S(1)} %get-tuple-element.7.codes, f32[3,2,2,2,256]{4,3,2,1,0:T(2,128)S(1)} %get-tuple-element.8.scales, f32[6,256,256]{2,1,0:T(8,128)S(1)} %get-tuple-element.9.first, ...), custom_call_target="tpu_custom_call" | custom-call | tf_op jit(solution)/shard_map/finish/pallas_call | solution.py:525

commit v10 on v8

--- a/solution.py
+++ b/solution.py
@@ -412,10 +412,13 @@
         first_out[j] = jnp.where(early | late, BETA_ONE * moment[j] + (1.0 - BETA_ONE) * gradient, 0.0)
         second_out[j] = jnp.where(late, second_late[table[4, j]], jnp.where(early, second_out[j], 0.0))
 
-    for s in range(slots):
-        for side in sides:
+    def give_near(order):
+        for s, side in order:
             pl.when(side["has"])(near(s // WAVE, side, s % WAVE).wait_recv)
             give(side["at"], s).start()
+
+    pl.when(left_edge)(lambda: give_near([(s, side) for side in (to_left, to_right) for s in range(slots)]))
+    pl.when(~left_edge)(lambda: give_near([(s, side) for s in range(slots) for side in sides]))
     for side in sides:
         pl.when(side["has"])(near_scale(side).wait_recv)
     give_scale().start()

time: 42.6 us -> 42.5 us (level)
  no operation moved by 1% of the time
where the time goes in v10:
time: 42.5 us; the launch traced here: 42.4 us
  Pallas kernels  41.7 us (98%)
  between operations  0.64 us (2%)
    pallas_call x1, Pallas kernels, body(): pl.pallas_call(functools.partial(soap_kernel, devices), out_shape=[pltpu....  39.7 us
    pallas_call x1, Pallas kernels, body(): pl.pallas_call(finish_kernel, out_shape=[jax.ShapeDtypeStruct((slots, wid...  2.05 us

profile of v10, /device:TPU:129, one launch (start us, length us, event | category | flops | bytes accessed | tf_op | source)
XLA Modules:
  0.0 42.4 jit_solution(11722143235689387632)
XLA Ops:
  0.6 39.7 %soap.1 = (f32[6,256,256]{2,1,0:T(8,128)S(1)}, f32[6,256,256]{2,1,0:T(8,128)S(1)}, s16[3,4,256,256]{3,2,1,0:T(8,128)(2,1)S(1)}, f32[3,2,2,2,256]{4,3,2,1,0:T(2,128)S(1)}) custom-call(s32[128]{0:T(128)} %starts_in.1, s32[384]{0:T(512)} %owners_in.1, bf16[1,4,256,256]{3,2,1,0:T(8,128)(2,1)} %grad.1, f32[6,256,256]{2,1,0:T(8,128)} %moment_in.1, ...), custom_call_target="tpu_custom_call" | custom-call | tf_op jit(solution)/shard_map/soap/pallas_call | solution.py:485
  40.3 2.0 %finish.1 = (f32[4,256,256]{2,1,0:T(8,128)}, f32[6,256,256]{2,1,0:T(8,128)}, f32[6,256,256]{2,1,0:T(8,128)}) custom-call(s16[3,4,256,256]{3,2,1,0:T(8,128)(2,1)S(1)} %get-tuple-element.7.codes, f32[3,2,2,2,256]{4,3,2,1,0:T(2,128)S(1)} %get-tuple-element.8.scales, f32[6,256,256]{2,1,0:T(8,128)S(1)} %get-tuple-element.9.first, ...), custom_call_target="tpu_custom_call" | custom-call | tf_op jit(solution)/shard_map/finish/pallas_call | solution.py:525
